TPU v7x, 32 devices: a whole 2x2x4 slice. The times are simulated.
32 devices in a mesh: row: 8 (over y, x, core), col: 4 (over z).
Axes of the slice: x: 2, y: 2, z: 4, core: 2. Of those that a mesh axis runs over, the one named last changes fastest.
Arguments:
- vectors_window: float32 [32, 8, 64, 1024], P(None, 'row', None, 'col'), may hold values from -6 to 6
- column_strip: float32 [32, 8, 64, 1024], P(None, 'row', None, 'col'), may hold values from -6 to 6
- row_strip: float32 [1024, 32, 4, 128], P('row', None, 'col'), may hold values from -6 to 6
- factor: float32 [1024, 1024], P('row', 'col'), may hold values from -2 to 2
- window_start: int32 [1], replicated, may hold values from 1 to 15360
- deflated: int32 [1], replicated, may hold values from 0 to 512
Outputs:
- vectors_updated: float32 [32, 8, 64, 1024], P(None, 'row', None, 'col')
- column_updated: float32 [32, 8, 64, 1024], P(None, 'row', None, 'col')
- row_updated: float32 [1024, 32, 4, 128], P('row', None, 'col')
All inputs are finite; a program needn't handle non-finite values.
Results may differ from a plain program's by a relative error of at most 0.0003.
Values sent between devices are 32-bit elements; how exact they have to be, the bound alone decides.
No kernel may reach another device: no remote copies, remote signals or barrier semaphores. Data moves between devices by JAX's collectives and lax.ppermute only.
A program may use at most 64 MiB of HBM per device.

v0:
```python
import functools

import jax
import jax.numpy as jnp
from jax import lax
from jax.experimental import pallas as pl
from jax.experimental.pallas import tpu as pltpu
from jax.sharding import PartitionSpec as P


LEVELS = 60
TILE = 256
VMEM_LIMIT = 48 * 1024 * 1024
VMEM = pl.BlockSpec(memory_space=pltpu.VMEM)
SMEM = pl.BlockSpec(memory_space=pltpu.SMEM)
ANY = pl.BlockSpec(memory_space=pl.ANY)
F32 = jnp.float32
BF16 = jnp.bfloat16


def exchange(value, axis, bits, size):
    return lax.ppermute(value, axis, [(i, i ^ bits) for i in range(size)])


def split(value):
    high = value.astype(BF16)
    return high, (value - high.astype(F32)).astype(BF16)


def dot(a, b):
    return jnp.dot(a, b, preferred_element_type=F32)


def gather_factor(factor, n_row, n_col):
    blocks = [factor] + [None] * (n_col - 1)
    for bits in range(n_col - 1, 0, -1):
        if bits == (n_col - 1) ^ 1 and n_col > 2:
            continue
        blocks[bits] = exchange(factor, "col", bits, n_col)
    if n_col > 2:
        blocks[(n_col - 1) ^ 1] = exchange(blocks[n_col - 1], "col", 1, n_col)
    own = jnp.stack(blocks)
    pieces = [(own, 0, 0)]
    bits = 1
    while bits < n_row:
        bits *= 2
    if bits == 8 and n_col % 2 == 0:
        half = n_col // 2
        x_side = exchange(own, "row", 2, n_row)
        y_side = exchange(own, "row", 4, n_row)
        first = exchange(y_side[:half], "row", 2, n_row)
        second = exchange(x_side[half:], "row", 4, n_row)
        pieces += [(x_side, 2, 0), (y_side, 4, 0), (first, 6, 0), (second, 6, half)]
    else:
        step = 2
        while step < n_row:
            pieces += [(exchange(a, "row", step, n_row), r ^ step, k) for a, r, k in pieces]
            step *= 2
    if n_row > 1:
        pieces += [(exchange(a, "row", 1, n_row), r ^ 1, k) for a, r, k in pieces]
    return pieces


def reflect_kernel(places, block_rows, scalars, *refs):
    count = len(places)
    sources = refs[:count]
    high_ref, low_ref = refs[count : count + 2]
    (vector_ref,) = refs[count + 2 :]
    row_position, col_position, kept_count = scalars[0], scalars[1], scalars[2]
    n_col, _, local_width = high_ref.shape
    groups = {}
    for source, (row_bits, col_bits) in zip(sources, places):
        groups.setdefault(row_bits, []).append((source, col_bits))
    for row_bits, members in groups.items():

        @pl.when(row_position == row_bits)
        def _():
            for source, col_bits in members:
                for k in range(source.shape[0]):
                    vector_ref[col_position ^ (col_bits + k)] = source[k, 0:1, :]

    corner = vector_ref[0, 0:1, 0:1]
    lane = lax.broadcasted_iota(jnp.int32, (1, local_width), 1)
    squares = jnp.zeros((1, 1), F32)
    for j in range(n_col):
        spike = jnp.where(lane + j * local_width < kept_count, vector_ref[j], 0.0)
        vector_ref[j] = spike
        squares = squares + jnp.sum(spike * spike, axis=1, keepdims=True)
    magnitude = jnp.sqrt(squares + 1e-06)
    signum = jnp.where(corner >= 0, 1.0, -1.0)
    vector_ref[0] = vector_ref[0] + jnp.where(lane == 0, signum * magnitude, 0.0)
    denominator = squares + 2.0 * jnp.abs(corner) * magnitude + magnitude * magnitude
    scaling = 2.0 / denominator
    for row_bits, members in groups.items():
        rows = pl.ds(pl.multiple_of((row_position ^ row_bits) * block_rows, block_rows), block_rows)
        image = jnp.zeros((block_rows, local_width), F32)
        for source, col_bits in members:

            def image_step(k, total):
                return total + source[k] * vector_ref[col_position ^ (col_bits + k)]

            image = lax.fori_loop(0, source.shape[0], image_step, image)
        image = jnp.sum(image, axis=1, keepdims=True) * scaling
        for source, col_bits in members:

            def write_step(k, carry):
                column = col_position ^ (col_bits + k)
                high, low = split(source[k] - image * vector_ref[column])
                high_ref[column, rows, :] = high
                low_ref[column, rows, :] = low
                return carry

            lax.fori_loop(0, source.shape[0], write_step, 0)


def reflect(pieces, scalars, n_row, n_col, block_rows, local_width):
    natural = jax.ShapeDtypeStruct((n_col, n_row * block_rows, local_width), BF16)
    return pl.pallas_call(
        functools.partial(reflect_kernel, [(r, k) for _, r, k in pieces], block_rows),
        in_specs=[SMEM] + [VMEM] * len(pieces),
        out_specs=[VMEM] * 2,
        out_shape=[natural, natural],
        scratch_shapes=[pltpu.VMEM((n_col, 1, local_width), F32)],
        compiler_params=pltpu.CompilerParams(vmem_limit_bytes=VMEM_LIMIT),
        name="reflect",
    )(scalars, *[a for a, _, _ in pieces])


def turn_kernel(masked, n_col, scalars, *refs):
    sources = refs[:n_col]
    high_ref, low_ref = refs[n_col : n_col + 2]
    outs = refs[n_col + 2 : 2 * n_col + 2]
    stacked, result = refs[2 * n_col + 2 :]
    position, threshold = scalars[0], scalars[1]
    rows, local_width = sources[0].shape
    for k in range(n_col):
        high, low = split(sources[k][...])
        stacked[position ^ k, :rows, :] = high
        stacked[position ^ k, rows:, :] = low

    def column_step(j, carry):
        column = position ^ j
        total = jnp.zeros((rows, local_width), F32)
        for k in range(n_col):
            band = pl.ds(k * local_width, local_width)
            both = dot(stacked[k], high_ref[column, band, :])
            total = total + both[rows:] + dot(stacked[k, :rows, :], low_ref[column, band, :]) + both[:rows]
        result[j] = total
        return carry

    lax.fori_loop(0, n_col, column_step, 0)
    for k in range(n_col):
        turned = result[k]
        if masked:
            number = lax.broadcasted_iota(jnp.int32, (rows, local_width), 0)
            turned = jnp.where(number < threshold, turned, sources[k][...])
        outs[k][...] = turned


def turn(sources, high, low, scalars, masked):
    n_col = len(sources)
    rows, local_width = sources[0].shape
    return pl.pallas_call(
        functools.partial(turn_kernel, masked, n_col),
        in_specs=[SMEM] + [VMEM] * (n_col + 2),
        out_specs=[VMEM] * n_col,
        out_shape=[jax.ShapeDtypeStruct((rows, local_width), F32)] * n_col,
        scratch_shapes=[
            pltpu.VMEM((n_col, 2 * rows, local_width), BF16),
            pltpu.VMEM((n_col, rows, local_width), F32),
        ],
        compiler_params=pltpu.CompilerParams(vmem_limit_bytes=VMEM_LIMIT),
        name="turn",
    )(scalars, *sources, high, low)


def stand_kernel(n_row, count, scalars, *refs):
    sources = refs[:n_row]
    high_ref, low_ref = refs[n_row : n_row + 2]
    outs = refs[n_row + 2 : 2 * n_row + 2]
    panel_high, panel_low, result = refs[2 * n_row + 2 :]
    position, threshold = scalars[0], scalars[1]
    n_col, width, local_width = high_ref.shape
    lanes = sources[0].shape[1]
    block_rows = sources[0].shape[0] // count
    for i in range(n_row):
        rows = pl.ds(pl.multiple_of((position ^ i) * block_rows, block_rows), block_rows)
        for t in range(count):
            high, low = split(sources[i][pl.ds(t, block_rows, stride=count), :])
            panel_high[rows, t * lanes : (t + 1) * lanes] = high
            panel_low[rows, t * lanes : (t + 1) * lanes] = low

    def rows_step(j, carry):
        total = jnp.zeros((local_width, count * lanes), F32)
        for k in range(width // TILE):
            band = pl.ds(k * TILE, TILE)
            left = high_ref[j, band, :].T
            total = total + dot(left, panel_low[band, :]) + dot(low_ref[j, band, :].T, panel_high[band, :])
            total = total + dot(left, panel_high[band, :])
        result[pl.ds(pl.multiple_of(j * local_width, local_width), local_width), :] = total
        return carry

    lax.fori_loop(0, n_col, rows_step, 0)
    lane = lax.broadcasted_iota(jnp.int32, (block_rows, lanes), 1)
    for i in range(n_row):
        rows = pl.ds(pl.multiple_of((position ^ i) * block_rows, block_rows), block_rows)
        for t in range(count):
            strided = pl.ds(t, block_rows, stride=count)
            outs[i][strided, :] = jnp.where(
                lane + t * lanes >= threshold,
                result[rows, t * lanes : (t + 1) * lanes],
                sources[i][strided, :],
            )


def stand(sources, high, low, scalars, count):
    n_row = len(sources)
    shape = sources[0].shape
    width = high.shape[1]
    return pl.pallas_call(
        functools.partial(stand_kernel, n_row, count),
        in_specs=[SMEM] + [VMEM] * (n_row + 2),
        out_specs=[VMEM] * n_row,
        out_shape=[jax.ShapeDtypeStruct(shape, F32)] * n_row,
        scratch_shapes=[
            pltpu.VMEM((width, count * shape[1]), BF16),
            pltpu.VMEM((width, count * shape[1]), BF16),
            pltpu.VMEM((width, count * shape[1]), F32),
        ],
        compiler_params=pltpu.CompilerParams(vmem_limit_bytes=VMEM_LIMIT),
        name="stand",
    )(scalars, *sources, high, low)


def place_kernel(groups, axis, tail, scalars, *refs):
    count = sum(len(g) for g in groups)
    pieces = refs[:count]
    position = scalars[0]
    if tail is None:
        target, sems = refs[count:]
    else:
        source, target, sems, kept, tail_sem = refs[count:]
        keep = pl.ds(tail, target.shape[0] - tail)
        fetch = pltpu.make_async_copy(source.at[keep], kept, tail_sem)
        fetch.start()
    copies = []
    for piece, (base, bits) in zip(pieces, [p for g in groups for p in g]):
        size = piece.shape[axis]
        start = base + (position ^ bits) * size
        if axis == 0 and size % 8 == 0 and base % 8 == 0:
            start = pl.multiple_of(start, 8)
        spot = (slice(None),) * axis + (pl.ds(start, size),)
        copies.append(pltpu.make_async_copy(piece, target.at[spot], sems.at[len(copies)]))
    for copy in copies:
        copy.start()
    if tail is not None:
        fetch.wait()
        copies.append(pltpu.make_async_copy(kept, target.at[keep], sems.at[len(copies)]))
        copies[-1].start()
    for copy in copies:
        copy.wait()


def place(groups, pieces, position, shape, axis=0, source=None, tail=None):
    operands = list(pieces)
    in_specs = [SMEM] + [VMEM] * len(pieces)
    scratch = [pltpu.SemaphoreType.DMA((len(pieces) + 1,))]
    if tail is not None:
        operands.append(source)
        in_specs.append(ANY)
        scratch += [pltpu.VMEM((shape[0] - tail,) + shape[1:], F32), pltpu.SemaphoreType.DMA]
    return pl.pallas_call(
        functools.partial(place_kernel, groups, axis, tail),
        in_specs=in_specs,
        out_specs=ANY,
        out_shape=jax.ShapeDtypeStruct(shape, F32),
        scratch_shapes=scratch,
        compiler_params=pltpu.CompilerParams(vmem_limit_bytes=VMEM_LIMIT),
        name="place",
    )(position, *operands)


def below(bound, period, block, position):
    full = bound // period
    return full * block + jnp.clip(bound - full * period - position * block, 0, block)


def body(n_row, n_col, vectors_window, column_strip, row_strip, factor, window_start, deflated):
    row_position = lax.axis_index("row").astype(jnp.int32)
    col_position = lax.axis_index("col").astype(jnp.int32)
    start_row = window_start[0]
    rounds, _, blocks, local_width = vectors_window.shape
    block_rows = factor.shape[0]
    width = block_rows * n_row
    strip_rows, col_rounds, _, col_block = row_strip.shape
    height = rounds * blocks
    vectors = vectors_window.reshape(height, local_width)
    strip = column_strip.reshape(height, local_width)

    pieces = gather_factor(factor, n_row, n_col)

    def rows_in(matrix, base, size):
        parts = [lax.dynamic_slice_in_dim(matrix, base + (col_position ^ k) * size, size) for k in range(n_col)]
        order = range(n_col - 1, 0, -1)
        got = {k: exchange(parts[k], "col", k, n_col) for k in order}
        return [parts[0]] + [got[k] for k in range(1, n_col)]

    def rows_out(parts):
        got = {k: exchange(parts[k], "col", k, n_col) for k in range(n_col - 1, 0, -1)}
        return [parts[0]] + [got[k] for k in range(1, n_col)]

    half = height // 2
    share = half // n_col
    first_in = rows_in(vectors, 0, share)
    second_in = rows_in(vectors, half, share)
    per_device = col_rounds // n_row
    piece_shape = (strip_rows, per_device, 1, col_block)
    flat_shape = (strip_rows * per_device, col_block)
    row_parts = [
        lax.dynamic_slice_in_dim(row_strip, (row_position ^ i) * per_device, per_device, axis=1).reshape(flat_shape)
        for i in range(n_row)
    ]
    row_in = [row_parts[0]] + [exchange(row_parts[i], "row", i, n_row) for i in range(1, n_row)]

    scalars = jnp.stack([row_position, col_position, width - deflated[0]])
    high, low = reflect(pieces, scalars, n_row, n_col, block_rows, local_width)

    col_scalars = jnp.stack([col_position, jnp.int32(0)])
    first_turned = turn(first_in, high, low, col_scalars, False)
    first_out = rows_out(first_turned)
    second_turned = turn(second_in, high, low, col_scalars, False)

    columns_kept = below(start_row + width, n_col * col_block, col_block, col_position)
    row_scalars = jnp.stack([row_position, columns_kept - row_position * (per_device * col_block)])
    stood = stand(row_in, high, low, row_scalars, per_device)
    row_out = [stood[0]] + [exchange(stood[i], "row", i, n_row) for i in range(1, n_row)]

    round_rows = n_row * blocks
    active_rounds = -(-(rounds * round_rows - width) // round_rows)
    levels = min(LEVELS // n_col, active_rounds)
    rows_turned = below(start_row, round_rows, blocks, row_position)
    sizes = [-(-active_rounds * (level + 1) // levels) for level in range(levels)]

    def branch(index, strip, high, low, rows_turned, *second):
        used = sizes[index]
        size = used * blocks // n_col
        strip_in = rows_in(strip, 0, size)
        second_out = rows_out(list(second))
        strip_scalars = jnp.stack([col_position, rows_turned - col_position * size])
        turned = turn(strip_in, high, low, strip_scalars, True)
        strip_out = rows_out(turned)
        groups = [[(0, k) for k in range(n_col)]]
        tail = used * blocks if used < rounds else None
        updated = place(groups, strip_out, col_scalars, strip.shape, source=strip, tail=tail)
        return [updated] + second_out

    used_rounds = -(-start_row // round_rows)
    level = sum((used_rounds > size).astype(jnp.int32) for size in sizes[:-1]) if levels > 1 else jnp.int32(0)
    strip_updated, *second_out = lax.switch(
        level, [functools.partial(branch, i) for i in range(levels)], strip, high, low, rows_turned, *second_turned
    )
    groups = [[(0, k) for k in range(n_col)], [(half, k) for k in range(n_col)]]
    vectors_updated = place(groups, first_out + second_out, col_scalars, vectors.shape)
    row_pieces = [part.reshape(piece_shape) for part in row_out]
    row_updated = place([[(0, i) for i in range(n_row)]], row_pieces, row_scalars, row_strip.shape, axis=1)
    return (
        vectors_updated.reshape(vectors_window.shape),
        strip_updated.reshape(column_strip.shape),
        row_updated,
    )


def solution(mesh):
    n_row, n_col = mesh.shape["row"], mesh.shape["col"]
    return jax.shard_map(
        functools.partial(body, n_row, n_col),
        mesh=mesh,
        in_specs=(
            P(None, "row", None, "col"),
            P(None, "row", None, "col"),
            P("row", None, "col", None),
            P("row", "col"),
            P(),
            P(),
        ),
        out_specs=(
            P(None, "row", None, "col"),
            P(None, "row", None, "col"),
            P("row", None, "col", None),
        ),
        check_vma=False,
    )
```

profile of v0, /device:TPU:0, one launch (start us, length us, event | category | flops | bytes accessed | tf_op | source)
XLA Modules:
  0.0 205.5 jit_solution(15937790623412724788)
XLA Ops:
  0.6 5.1 %collective-permute-start.139 = (f32[128,256]{1,0:T(8,128)}, f32[128,256]{1,0:T(8,128)S(1)}, u32[]{:S(2)}, u32[]{:S(2)}) collective-permute-start(f32[128,256]{1,0:T(8,128)} %param.24), channel_id=1, source_target_pairs={{0,3},{1,2},{2,1},{3,0},{4,7},{5,6},{6,5},{7,4},{8,11},{9,10},{10,... | collective-permute-start | bytes 393224 | tf_op jit(solution)/shard_map/ppermute | solution.py:22
  5.8 4.6 %collective-permute-done.139 = f32[128,256]{1,0:T(8,128)S(1)} collective-permute-done((f32[128,256]{1,0:T(8,128)}, f32[128,256]{1,0:T(8,128)S(1)}, u32[]{:S(2)}, u32[]{:S(2)}) %collective-permute-start.139) | collective-permute-done | bytes 131104 | tf_op jit(solution)/shard_map/ppermute | solution.py:22
  10.4 1.6 collective-permute-start.140
  12.8 2.6 %collective-permute-done.140 = f32[128,256]{1,0:T(8,128)S(1)} collective-permute-done((f32[128,256]{1,0:T(8,128)S(1)}, f32[128,256]{1,0:T(8,128)S(1)}, u32[]{:S(2)}, u32[]{:S(2)}) %collective-permute-start.140) | collective-permute-done | bytes 131104 | tf_op jit(solution)/shard_map/ppermute | solution.py:22
  16.3 1.7 collective-permute-start.141
  18.0 1.5 collective-permute-start.142
  19.5 8.9 %collective-permute-done.141.refs_1_ = f32[4,128,256]{2,1,0:T(8,128)S(1)} collective-permute-done((f32[4,128,256]{2,1,0:T(8,128)S(1)}, f32[4,128,256]{2,1,0:T(8,128)S(1)}, u32[]{:S(2)}, u32[]{:S(2)}) %collective-permute-start.141) | collective-permute-done | bytes 524320 | tf_op jit(solution)/shard_map/ppermute | solution.py:22
  32.0 1.6 collective-permute-start.144
  33.7 2.6 %constant_dynamic-slice_fusion.68 = (f32[256,256]{1,0:T(8,128)S(1)}, f32[256,256]{1,0:T(8,128)S(1)}, f32[256,256]{1,0:T(8,128)S(1)}, f32[256,256]{1,0:T(8,128)S(...) fusion(f32[2048,256]{1,0:T(8,128)} %bitcast.192, ...), kind=kLoop, calls=%fused_computation.84 | loop fusion | bytes 4194336 | tf_op jit(solution)/shard_map/dynamic_slice | solution.py:303
  36.3 1.7 collective-permute-start.153
  38.0 1.9 collective-permute-done.143.refs_3_
  41.1 2.9 %collective-permute-start.155 = (f32[256,256]{1,0:T(8,128)S(1)}, f32[256,256]{1,0:T(8,128)S(1)}, u32[]{:S(2)}, u32[]{:S(2)}) collective-permute-start(f32[256,256]{1,0:T(8,128)S(1)} %get-tuple-element.1305), channel_id=1, source_target_pairs={{0,3},{1,2},{2,1},{3,0},{4,7},{5,6},{6,5},{7,4},{8,11},{9,10},{10,... | collective-permute-start | bytes 786440 | tf_op jit(solution)/shard_map/ppermute | solution.py:22
  44.6 2.5 %constant_dynamic-slice_fusion.60 = (f32[128,4,1,128]{3,2,1,0:T(1,128)}, f32[128,4,1,128]{3,2,1,0:T(1,128)}, f32[128,4,1,128]{3,2,1,0:T(1,128)}, f32[128,4,1,128...) fusion(f32[128,32,1,128]{3,2,1,0:T(1,128)S(1)} %copy-done.21, ...), kind=kLoop, calls=%fused_computation.76 | loop fusion | bytes 4194336 | tf_op jit(solution)/shard_map/dynamic_slice | solution.py:320
  47.1 7.9 %reflect.1 = (bf16[4,1024,256]{2,1,0:T(8,128)(2,1)}, bf16[4,1024,256]{2,1,0:T(8,128)(2,1)}) custom-call(s32[3]{0:T(128)S(1)} %pad_add_fusion.16.scalars, f32[4,128,256]{2,1,0:T(8,128)S(1)} %pad_maximum_fusion.refs_0_, f32[4,128,256]{2,1,0:T(8,128)S(1)} %collective-permute-done.141.refs_1_, f32[4,128,256]{2,1,0:T(8,128)S(1)} %collective-permute-done.142.refs_2_, ...), custom_call_target="tpu_custom_call" | custom-call | tf_op jit(solution)/shard_map/reflect/pallas_call | solution.py:118
  55.0 6.2 %collective-permute-done.154.refs_2_ = f32[256,256]{1,0:T(8,128)S(1)} collective-permute-done((f32[256,256]{1,0:T(8,128)S(1)}, f32[256,256]{1,0:T(8,128)S(1)}, u32[]{:S(2)}, u32[]{:S(2)}) %collective-permute-start.154) | collective-permute-done | bytes 262176 | tf_op jit(solution)/shard_map/ppermute | solution.py:22
  61.2 5.8 %turn.33 = (f32[256,256]{1,0:T(8,128)S(1)}, f32[256,256]{1,0:T(8,128)}, f32[256,256]{1,0:T(8,128)}, f32[256,256]{1,0:T(8,128)}) custom-call(s32[2]{0:T(128)S(1)} %pad_add_fusion.15.scalars, f32[256,256]{1,0:T(8,128)S(1)} %get-tuple-element.1308.refs_0_, f32[256,256]{1,0:T(8,128)S(1)} %collective-permute-done.153.refs_1_, ...), custom_call_target="tpu_custom_call" | custom-call | tf_op jit(solution)/shard_map/turn/pallas_call | solution.py:163
  67.0 61.2 %conditional.1 = (f32[256,256]{1,0:T(8,128)}, f32[256,256]{1,0:T(8,128)}, f32[256,256]{1,0:T(8,128)}, f32[32,1,64,256]{3,2,1,0:T(8,128)}) conditional(s32[]{:T(128)} %clamp.3, (f32[256,256]{1,0:T(8,128)}, f32[256,256]{1,0:T(8,128)}, f32[256,256]{1,0:T(8,128)}, s32[]{:T(128)}, s32[]{:T(128)}, /*index=5*/s32[]{:T(128)}, ...), branch_computations={%region_0.1_spmd, %region_1.2_spmd, %region_2.3_spmd, %region_3.4_... | conditional | flops 38 | bytes 38798280 | solution.py:359
  67.7 5.0 %collective-permute-start.30 = (f32[128,256]{1,0:T(8,128)}, f32[128,256]{1,0:T(8,128)S(1)}, u32[]{:S(2)}, u32[]{:S(2)}) collective-permute-start(f32[128,256]{1,0:T(8,128)} %get-tuple-element.1251), channel_id=1, source_target_pairs={{0,1},{1,0},{2,3},{3,2},{4,5},{5,4},{6,7},{7,6},{8,9},{9,8},{10,11... | collective-permute-start | bytes 393224 | tf_op jit(solution)/shard_map/cond/branch_3_fun/ppermute | solution.py:22
  73.5 1.5 collective-permute-start.32
  77.1 7.8 %collective-permute-done.31.refs_2_ = f32[128,256]{1,0:T(8,128)S(1)} collective-permute-done((f32[128,256]{1,0:T(8,128)}, f32[128,256]{1,0:T(8,128)S(1)}, u32[]{:S(2)}, u32[]{:S(2)}) %collective-permute-start.31) | collective-permute-done | bytes 131104 | tf_op jit(solution)/shard_map/cond/branch_3_fun/ppermute | solution.py:22
  84.9 3.9 %turn.20 = (f32[128,256]{1,0:T(8,128)S(1)}, f32[128,256]{1,0:T(8,128)S(1)}, f32[128,256]{1,0:T(8,128)S(1)}, f32[128,256]{1,0:T(8,128)S(1)}) custom-call(s32[2]{0:T(128)S(1)} %pad_add_fusion.3.scalars, f32[128,256]{1,0:T(8,128)S(1)} %get-tuple-element.1252.refs_0_, f32[128,256]{1,0:T(8,128)S(1)} %collective-permute-done.30.refs_1_, ...), custom_call_target="tpu_custom_call" | custom-call | tf_op jit(solution)/shard_map/cond/branch_3_fun/turn/pallas_call | solution.py:163
  88.8 2.1 %collective-permute-start.33 = (f32[128,256]{1,0:T(8,128)S(1)}, f32[128,256]{1,0:T(8,128)S(1)}, u32[]{:S(2)}, u32[]{:S(2)}) collective-permute-start(f32[128,256]{1,0:T(8,128)S(1)} %get-tuple-element.613), channel_id=1, source_target_pairs={{0,1},{1,0},{2,3},{3,2},{4,5},{5,4},{6,7},{7,6},{8,9},{9,8},{10,11... | collective-permute-start | bytes 393224 | tf_op jit(solution)/shard_map/cond/branch_3_fun/ppermute | solution.py:22
  91.0 2.8 %collective-permute-start.28 = (f32[256,256]{1,0:T(8,128)S(1)}, f32[256,256]{1,0:T(8,128)}, u32[]{:S(2)}, u32[]{:S(2)}) collective-permute-start(f32[256,256]{1,0:T(8,128)S(1)} %copy-done.32), channel_id=1, source_target_pairs={{0,2},{1,3},{2,0},{3,1},{4,6},{5,7},{6,4},{7,5},{8,10},{9,11},{10,... | collective-permute-start | bytes 786440 | tf_op jit(solution)/shard_map/cond/branch_3_fun/ppermute | solution.py:22
  93.8 1.5 collective-permute-start.29
  95.3 5.0 %collective-permute-done.33.refs_1_ = f32[128,256]{1,0:T(8,128)S(1)} collective-permute-done((f32[128,256]{1,0:T(8,128)S(1)}, f32[128,256]{1,0:T(8,128)S(1)}, u32[]{:S(2)}, u32[]{:S(2)}) %collective-permute-start.33) | collective-permute-done | bytes 131104 | tf_op jit(solution)/shard_map/cond/branch_3_fun/ppermute | solution.py:22
  100.3 1.7 collective-permute-start.35
  102.1 23.5 %collective-permute-done.34.refs_2_ = f32[128,256]{1,0:T(8,128)S(1)} collective-permute-done((f32[128,256]{1,0:T(8,128)S(1)}, f32[128,256]{1,0:T(8,128)S(1)}, u32[]{:S(2)}, u32[]{:S(2)}) %collective-permute-start.34) | collective-permute-done | bytes 131104 | tf_op jit(solution)/shard_map/cond/branch_3_fun/ppermute | solution.py:22
  125.6 2.0 place.20
  128.3 1.8 collective-permute-start.158
  130.1 2.1 collective-permute-start.159
  132.2 1.2 collective-permute-start.161
  133.4 4.3 %collective-permute-done.157.refs_2_ = f32[512,128]{1,0:T(8,128)S(1)} collective-permute-done((f32[512,128]{1,0:T(8,128)}, f32[512,128]{1,0:T(8,128)S(1)}, u32[]{:S(2)}, u32[]{:S(2)}) %collective-permute-start.157) | collective-permute-done | bytes 262176 | tf_op jit(solution)/shard_map/ppermute | solution.py:22
  138.4 3.8 %collective-permute-done.158.refs_3_ = f32[512,128]{1,0:T(8,128)S(1)} collective-permute-done((f32[512,128]{1,0:T(8,128)}, f32[512,128]{1,0:T(8,128)S(1)}, u32[]{:S(2)}, u32[]{:S(2)}) %collective-permute-start.158) | collective-permute-done | bytes 262176 | tf_op jit(solution)/shard_map/ppermute | solution.py:22
  142.2 2.0 collective-permute-start.135
  145.3 10.4 %collective-permute-done.160.refs_5_ = f32[512,128]{1,0:T(8,128)S(1)} collective-permute-done((f32[512,128]{1,0:T(8,128)}, f32[512,128]{1,0:T(8,128)S(1)}, u32[]{:S(2)}, u32[]{:S(2)}) %collective-permute-start.160) | collective-permute-done | bytes 262176 | tf_op jit(solution)/shard_map/ppermute | solution.py:22
  155.7 2.4 %collective-permute-start.137 = (f32[256,256]{1,0:T(8,128)}, f32[256,256]{1,0:T(8,128)}, u32[]{:S(2)}, u32[]{:S(2)}) collective-permute-start(f32[256,256]{1,0:T(8,128)} %get-tuple-element.1309), channel_id=1, source_target_pairs={{0,3},{1,2},{2,1},{3,0},{4,7},{5,6},{6,5},{7,4},{8,11},{9,10},{10,... | collective-permute-start | bytes 786440 | tf_op jit(solution)/shard_map/ppermute | solution.py:22
  158.2 6.8 %stand.1 = (f32[512,128]{1,0:T(8,128)S(1)}, f32[512,128]{1,0:T(8,128)S(1)}, f32[512,128]{1,0:T(8,128)S(1)}, f32[512,128]{1,0:T(8,128)S(1)}, f32[512,128]{1,0:T(8...) custom-call(s32[2]{0:T(128)S(1)} %pad_add_fusion.17.scalars, ...), custom_call_target="tpu_custom_call" | custom-call | tf_op jit(solution)/shard_map/stand/pallas_call | solution.py:220
  165.4 1.6 collective-permute-start.165
  167.0 1.5 collective-permute-start.166
  170.1 4.4 %collective-permute-done.164 = f32[512,128]{1,0:T(8,128)S(1)} collective-permute-done((f32[512,128]{1,0:T(8,128)S(1)}, f32[512,128]{1,0:T(8,128)S(1)}, u32[]{:S(2)}, u32[]{:S(2)}) %collective-permute-start.164) | collective-permute-done | bytes 262176 | tf_op jit(solution)/shard_map/ppermute | solution.py:22
  174.5 4.8 %turn.32 = (f32[256,256]{1,0:T(8,128)S(1)}, f32[256,256]{1,0:T(8,128)S(1)}, f32[256,256]{1,0:T(8,128)S(1)}, f32[256,256]{1,0:T(8,128)S(1)}) custom-call(s32[2]{0:T(128)S(1)} %pad_add_fusion.15.scalars, f32[256,256]{1,0:T(8,128)S(1)} %get-tuple-element.1312.refs_0_, f32[256,256]{1,0:T(8,128)S(1)} %collective-permute-done.135.refs_1_, ...), custom_call_target="tpu_custom_call" | custom-call | tf_op jit(solution)/shard_map/turn/pallas_call | solution.py:163
  179.3 2.0 collective-permute-start.150
  182.4 9.5 %collective-permute-done.167 = f32[512,128]{1,0:T(8,128)S(1)} collective-permute-done((f32[512,128]{1,0:T(8,128)S(1)}, f32[512,128]{1,0:T(8,128)S(1)}, u32[]{:S(2)}, u32[]{:S(2)}) %collective-permute-start.167) | collective-permute-done | bytes 262176 | tf_op jit(solution)/shard_map/ppermute | solution.py:22
  192.0 1.4 collective-permute-start.152
  193.4 1.9 place.33
  195.3 1.4 collective-permute-done.151.refs_2_
  196.7 6.0 %collective-permute-done.152.refs_3_ = f32[256,256]{1,0:T(8,128)S(1)} collective-permute-done((f32[256,256]{1,0:T(8,128)S(1)}, f32[256,256]{1,0:T(8,128)S(1)}, u32[]{:S(2)}, u32[]{:S(2)}) %collective-permute-start.152) | collective-permute-done | bytes 262176 | tf_op jit(solution)/shard_map/ppermute | solution.py:22
  202.7 2.5 %place.32 = f32[2048,256]{1,0:T(8,128)} custom-call(s32[2]{0:T(128)S(1)} %pad_add_fusion.15.scalars, f32[256,256]{1,0:T(8,128)S(1)} %get-tuple-element.808.refs_0_, f32[256,256]{1,0:T(8,128)S(1)} %collective-permute-done.150.refs_1_, f32[256,256]{1,0:T(8,128)S(1)} %collective-permute-done.151.refs_2_, f32[256,256]{1,0:T(8,128)S(1)} %collective-permute-done.152.refs_3_, ...), custom_call_target="tpu_custom_call" | custom-call | tf_op jit(solution)/shard_map/place/pallas_call | solution.py:272
  (69 shorter events, 12.9 us)
Async XLA Ops:
  0.6 9.7 %collective-permute-start.139 = (f32[128,256]{1,0:T(8,128)}, f32[128,256]{1,0:T(8,128)S(1)}, u32[]{:S(2)}, u32[]{:S(2)}) collective-permute-start(f32[128,256]{1,0:T(8,128)} %param.24), channel_id=1, source_target_pairs={{0,3},{1,2},{2,1},{3,0},{4,7},{5,6},{6,5},{7,4},{8,11},{9,10},{10,... | collective-permute-start | bytes 393224 | tf_op jit(solution)/shard_map/ppermute | solution.py:22
  5.8 7.0 %collective-permute-start.138 = (f32[128,256]{1,0:T(8,128)}, f32[128,256]{1,0:T(8,128)S(1)}, u32[]{:S(2)}, u32[]{:S(2)}) collective-permute-start(f32[128,256]{1,0:T(8,128)} %param.24), channel_id=1, source_target_pairs={{0,1},{1,0},{2,3},{3,2},{4,5},{5,4},{6,7},{7,6},{8,9},{9,8},{10,11... | collective-permute-start | bytes 393224 | tf_op jit(solution)/shard_map/ppermute | solution.py:22
  10.4 5.0 %collective-permute-start.140 = (f32[128,256]{1,0:T(8,128)S(1)}, f32[128,256]{1,0:T(8,128)S(1)}, u32[]{:S(2)}, u32[]{:S(2)}) collective-permute-start(f32[128,256]{1,0:T(8,128)S(1)} %collective-permute-done.139), channel_id=1, source_target_pairs={{0,1},{1,0},{2,3},{3,2},{4,5},{5,4},{6,7},{7,6},{8,9},{9,8},{10,11... | collective-permute-start | bytes 393224 | tf_op jit(solution)/shard_map/ppermute | solution.py:22
  16.3 12.2 %collective-permute-start.141 = (f32[4,128,256]{2,1,0:T(8,128)S(1)}, f32[4,128,256]{2,1,0:T(8,128)S(1)}, u32[]{:S(2)}, u32[]{:S(2)}) collective-permute-start(f32[4,128,256]{2,1,0:T(8,128)S(1)} %pad_maximum_fusion.refs_0_), channel_id=1, source_target_pairs={{0,8},{4,12},{8,0},{12,4},{16,24},{20,28},{24,16},{28,20},{1,9},{5... | collective-permute-start | bytes 1572872 | tf_op jit(solution)/shard_map/ppermute | solution.py:22
  18.0 11.6 %collective-permute-start.142 = (f32[4,128,256]{2,1,0:T(8,128)S(1)}, f32[4,128,256]{2,1,0:T(8,128)S(1)}, u32[]{:S(2)}, u32[]{:S(2)}) collective-permute-start(f32[4,128,256]{2,1,0:T(8,128)S(1)} %pad_maximum_fusion.refs_0_), channel_id=1, source_target_pairs={{0,16},{4,20},{8,24},{12,28},{16,0},{20,4},{24,8},{28,12},{1,17},{... | collective-permute-start | bytes 1572872 | tf_op jit(solution)/shard_map/ppermute | solution.py:22
  19.5 16.8 %collective-permute-start.145 = (f32[4,128,256]{2,1,0:T(8,128)S(1)}, f32[4,128,256]{2,1,0:T(8,128)S(1)}, u32[]{:S(2)}, u32[]{:S(2)}) collective-permute-start(f32[4,128,256]{2,1,0:T(8,128)S(1)} %pad_maximum_fusion.refs_0_), channel_id=1, source_target_pairs={{0,4},{4,0},{8,12},{12,8},{16,20},{20,16},{24,28},{28,24},{1,5},{5... | collective-permute-start | bytes 1572872 | tf_op jit(solution)/shard_map/ppermute | solution.py:22
  28.5 15.5 %collective-permute-start.146 = (f32[4,128,256]{2,1,0:T(8,128)S(1)}, f32[4,128,256]{2,1,0:T(8,128)S(1)}, u32[]{:S(2)}, u32[]{:S(2)}) collective-permute-start(f32[4,128,256]{2,1,0:T(8,128)S(1)} %collective-permute-done.141.refs_1_), channel_id=1, source_target_pairs={{0,4},{4,0},{8,12},{12,8},{16,20},{20,16},{24,28},{28,24},{1,5},{5... | collective-permute-start | bytes 1572872 | tf_op jit(solution)/shard_map/ppermute | solution.py:22
  29.7 14.3 %collective-permute-start.147 = (f32[4,128,256]{2,1,0:T(8,128)S(1)}, f32[4,128,256]{2,1,0:T(8,128)}, u32[]{:S(2)}, u32[]{:S(2)}) collective-permute-start(f32[4,128,256]{2,1,0:T(8,128)S(1)} %collective-permute-done.142.refs_2_), channel_id=1, source_target_pairs={{0,4},{4,0},{8,12},{12,8},{16,20},{20,16},{24,28},{28,24},{1,5},{5... | collective-permute-start | bytes 1572872 | tf_op jit(solution)/shard_map/ppermute | solution.py:22
  31.2 8.8 %collective-permute-start.143 = (f32[2,128,256]{2,1,0:T(8,128)S(1)}, f32[2,128,256]{2,1,0:T(8,128)S(1)}, u32[]{:S(2)}, u32[]{:S(2)}) collective-permute-start(f32[2,128,256]{2,1,0:T(8,128)S(1)} %slice.8), channel_id=1, source_target_pairs={{0,8},{4,12},{8,0},{12,4},{16,24},{20,28},{24,16},{28,20},{1,9},{5... | collective-permute-start | bytes 786440 | tf_op jit(solution)/shard_map/ppermute | solution.py:22
  32.0 9.0 %collective-permute-start.144 = (f32[2,128,256]{2,1,0:T(8,128)S(1)}, f32[2,128,256]{2,1,0:T(8,128)S(1)}, u32[]{:S(2)}, u32[]{:S(2)}) collective-permute-start(f32[2,128,256]{2,1,0:T(8,128)S(1)} %slice.9), channel_id=1, source_target_pairs={{0,16},{4,20},{8,24},{12,28},{16,0},{20,4},{24,8},{28,12},{1,17},{... | collective-permute-start | bytes 786440 | tf_op jit(solution)/shard_map/ppermute | solution.py:22
  33.7 10.9 %copy-start.21 = (f32[128,32,1,128]{3,2,1,0:T(1,128)S(1)}, f32[128,32,1,128]{3,2,1,0:T(1,128)}, u32[]{:S(2)}) copy-start(f32[128,32,1,128]{3,2,1,0:T(1,128)} %param.23) | copy-start | bytes 6291460
  36.3 18.7 %collective-permute-start.153 = (f32[256,256]{1,0:T(8,128)S(1)}, f32[256,256]{1,0:T(8,128)S(1)}, u32[]{:S(2)}, u32[]{:S(2)}) collective-permute-start(f32[256,256]{1,0:T(8,128)S(1)} %get-tuple-element.1307), channel_id=1, source_target_pairs={{0,1},{1,0},{2,3},{3,2},{4,5},{5,4},{6,7},{7,6},{8,9},{9,8},{10,11... | collective-permute-start | bytes 786440 | tf_op jit(solution)/shard_map/ppermute | solution.py:22
  39.9 21.2 %collective-permute-start.154 = (f32[256,256]{1,0:T(8,128)S(1)}, f32[256,256]{1,0:T(8,128)S(1)}, u32[]{:S(2)}, u32[]{:S(2)}) collective-permute-start(f32[256,256]{1,0:T(8,128)S(1)} %get-tuple-element.1306), channel_id=1, source_target_pairs={{0,2},{1,3},{2,0},{3,1},{4,6},{5,7},{6,4},{7,5},{8,10},{9,11},{10,... | collective-permute-start | bytes 786440 | tf_op jit(solution)/shard_map/ppermute | solution.py:22
  41.1 20.1 %collective-permute-start.155 = (f32[256,256]{1,0:T(8,128)S(1)}, f32[256,256]{1,0:T(8,128)S(1)}, u32[]{:S(2)}, u32[]{:S(2)}) collective-permute-start(f32[256,256]{1,0:T(8,128)S(1)} %get-tuple-element.1305), channel_id=1, source_target_pairs={{0,3},{1,2},{2,1},{3,0},{4,7},{5,6},{6,5},{7,4},{8,11},{9,10},{10,... | collective-permute-start | bytes 786440 | tf_op jit(solution)/shard_map/ppermute | solution.py:22
  44.0 3.1 %collective-permute-start.148 = (f32[2,128,256]{2,1,0:T(8,128)S(1)}, f32[2,128,256]{2,1,0:T(8,128)S(1)}, u32[]{:S(2)}, u32[]{:S(2)}) collective-permute-start(f32[2,128,256]{2,1,0:T(8,128)S(1)} %collective-permute-done.143.refs_3_), channel_id=1, source_target_pairs={{0,4},{4,0},{8,12},{12,8},{16,20},{20,16},{24,28},{28,24},{1,5},{5... | collective-permute-start | bytes 786440 | tf_op jit(solution)/shard_map/ppermute | solution.py:22
  44.0 3.1 %collective-permute-start.149 = (f32[2,128,256]{2,1,0:T(8,128)S(1)}, f32[2,128,256]{2,1,0:T(8,128)S(1)}, u32[]{:S(2)}, u32[]{:S(2)}) collective-permute-start(f32[2,128,256]{2,1,0:T(8,128)S(1)} %collective-permute-done.144.refs_4_), channel_id=1, source_target_pairs={{0,4},{4,0},{8,12},{12,8},{16,20},{20,16},{24,28},{28,24},{1,5},{5... | collective-permute-start | bytes 786440 | tf_op jit(solution)/shard_map/ppermute | solution.py:22
  67.7 9.4 %collective-permute-start.30 = (f32[128,256]{1,0:T(8,128)}, f32[128,256]{1,0:T(8,128)S(1)}, u32[]{:S(2)}, u32[]{:S(2)}) collective-permute-start(f32[128,256]{1,0:T(8,128)} %get-tuple-element.1251), channel_id=1, source_target_pairs={{0,1},{1,0},{2,3},{3,2},{4,5},{5,4},{6,7},{7,6},{8,9},{9,8},{10,11... | collective-permute-start | bytes 393224 | tf_op jit(solution)/shard_map/cond/branch_3_fun/ppermute | solution.py:22
  72.7 12.2 %collective-permute-start.31 = (f32[128,256]{1,0:T(8,128)}, f32[128,256]{1,0:T(8,128)S(1)}, u32[]{:S(2)}, u32[]{:S(2)}) collective-permute-start(f32[128,256]{1,0:T(8,128)} %get-tuple-element.1250), channel_id=1, source_target_pairs={{0,2},{1,3},{2,0},{3,1},{4,6},{5,7},{6,4},{7,5},{8,10},{9,11},{10,... | collective-permute-start | bytes 393224 | tf_op jit(solution)/shard_map/cond/branch_3_fun/ppermute | solution.py:22
  73.5 11.4 %collective-permute-start.32 = (f32[128,256]{1,0:T(8,128)S(1)}, f32[128,256]{1,0:T(8,128)S(1)}, u32[]{:S(2)}, u32[]{:S(2)}) collective-permute-start(f32[128,256]{1,0:T(8,128)S(1)} %get-tuple-element.1249), channel_id=1, source_target_pairs={{0,3},{1,2},{2,1},{3,0},{4,7},{5,6},{6,5},{7,4},{8,11},{9,10},{10,... | collective-permute-start | bytes 393224 | tf_op jit(solution)/shard_map/cond/branch_3_fun/ppermute | solution.py:22
  84.9 6.0 %copy-start.22 = (f32[256,256]{1,0:T(8,128)S(1)}, f32[256,256]{1,0:T(8,128)}, u32[]{:S(2)}) copy-start(f32[256,256]{1,0:T(8,128)} %get-tuple-element.601) | copy-start | bytes 786436 | tf_op jit(solution)/shard_map/cond
  84.9 6.1 %copy-start.32 = (f32[256,256]{1,0:T(8,128)S(1)}, f32[256,256]{1,0:T(8,128)}, u32[]{:S(2)}) copy-start(f32[256,256]{1,0:T(8,128)} %get-tuple-element.602) | copy-start | bytes 786436 | tf_op jit(solution)/shard_map/cond
  84.9 8.9 %copy-start.42 = (f32[256,256]{1,0:T(8,128)S(1)}, f32[256,256]{1,0:T(8,128)}, u32[]{:S(2)}) copy-start(f32[256,256]{1,0:T(8,128)} %get-tuple-element.603) | copy-start | bytes 786436 | tf_op jit(solution)/shard_map/cond
  88.8 11.5 %collective-permute-start.33 = (f32[128,256]{1,0:T(8,128)S(1)}, f32[128,256]{1,0:T(8,128)S(1)}, u32[]{:S(2)}, u32[]{:S(2)}) collective-permute-start(f32[128,256]{1,0:T(8,128)S(1)} %get-tuple-element.613), channel_id=1, source_target_pairs={{0,1},{1,0},{2,3},{3,2},{4,5},{5,4},{6,7},{7,6},{8,9},{9,8},{10,11... | collective-permute-start | bytes 393224 | tf_op jit(solution)/shard_map/cond/branch_3_fun/ppermute | solution.py:22
  90.9 36.7 %collective-permute-start.27 = (f32[256,256]{1,0:T(8,128)S(1)}, f32[256,256]{1,0:T(8,128)}, u32[]{:S(2)}, u32[]{:S(2)}) collective-permute-start(f32[256,256]{1,0:T(8,128)S(1)} %copy-done.22), channel_id=1, source_target_pairs={{0,1},{1,0},{2,3},{3,2},{4,5},{5,4},{6,7},{7,6},{8,9},{9,8},{10,11... | collective-permute-start | bytes 786440 | tf_op jit(solution)/shard_map/cond/branch_3_fun/ppermute | solution.py:22
  91.0 36.6 %collective-permute-start.28 = (f32[256,256]{1,0:T(8,128)S(1)}, f32[256,256]{1,0:T(8,128)}, u32[]{:S(2)}, u32[]{:S(2)}) collective-permute-start(f32[256,256]{1,0:T(8,128)S(1)} %copy-done.32), channel_id=1, source_target_pairs={{0,2},{1,3},{2,0},{3,1},{4,6},{5,7},{6,4},{7,5},{8,10},{9,11},{10,... | collective-permute-start | bytes 786440 | tf_op jit(solution)/shard_map/cond/branch_3_fun/ppermute | solution.py:22
  93.8 33.9 %collective-permute-start.29 = (f32[256,256]{1,0:T(8,128)S(1)}, f32[256,256]{1,0:T(8,128)}, u32[]{:S(2)}, u32[]{:S(2)}) collective-permute-start(f32[256,256]{1,0:T(8,128)S(1)} %copy-done.42), channel_id=1, source_target_pairs={{0,3},{1,2},{2,1},{3,0},{4,7},{5,6},{6,5},{7,4},{8,11},{9,10},{10,... | collective-permute-start | bytes 786440 | tf_op jit(solution)/shard_map/cond/branch_3_fun/ppermute | solution.py:22
  95.3 30.3 %collective-permute-start.34 = (f32[128,256]{1,0:T(8,128)S(1)}, f32[128,256]{1,0:T(8,128)S(1)}, u32[]{:S(2)}, u32[]{:S(2)}) collective-permute-start(f32[128,256]{1,0:T(8,128)S(1)} %get-tuple-element.614), channel_id=1, source_target_pairs={{0,2},{1,3},{2,0},{3,1},{4,6},{5,7},{6,4},{7,5},{8,10},{9,11},{10,... | collective-permute-start | bytes 393224 | tf_op jit(solution)/shard_map/cond/branch_3_fun/ppermute | solution.py:22
  100.3 25.2 %collective-permute-start.35 = (f32[128,256]{1,0:T(8,128)S(1)}, f32[128,256]{1,0:T(8,128)S(1)}, u32[]{:S(2)}, u32[]{:S(2)}) collective-permute-start(f32[128,256]{1,0:T(8,128)S(1)} %get-tuple-element.615), channel_id=1, source_target_pairs={{0,3},{1,2},{2,1},{3,0},{4,7},{5,6},{6,5},{7,4},{8,11},{9,10},{10,... | collective-permute-start | bytes 393224 | tf_op jit(solution)/shard_map/cond/branch_3_fun/ppermute | solution.py:22
  128.2 4.0 %collective-permute-start.156 = (f32[512,128]{1,0:T(8,128)}, f32[512,128]{1,0:T(8,128)S(1)}, u32[]{:S(2)}, u32[]{:S(2)}) collective-permute-start(f32[512,128]{1,0:T(8,128)} %bitcast.200), channel_id=1, source_target_pairs={{0,4},{4,0},{8,12},{12,8},{16,20},{20,16},{24,28},{28,24},{1,5},{5... | collective-permute-start | bytes 786440 | tf_op jit(solution)/shard_map/ppermute | solution.py:22
  128.3 9.5 %collective-permute-start.157 = (f32[512,128]{1,0:T(8,128)}, f32[512,128]{1,0:T(8,128)S(1)}, u32[]{:S(2)}, u32[]{:S(2)}) collective-permute-start(f32[512,128]{1,0:T(8,128)} %bitcast.199), channel_id=1, source_target_pairs={{0,8},{4,12},{8,0},{12,4},{16,24},{20,28},{24,16},{28,20},{1,9},{5... | collective-permute-start | bytes 786440 | tf_op jit(solution)/shard_map/ppermute | solution.py:22
  128.3 13.9 %collective-permute-start.158 = (f32[512,128]{1,0:T(8,128)}, f32[512,128]{1,0:T(8,128)S(1)}, u32[]{:S(2)}, u32[]{:S(2)}) collective-permute-start(f32[512,128]{1,0:T(8,128)} %bitcast.198), channel_id=1, source_target_pairs={{0,12},{4,8},{8,4},{12,0},{16,28},{20,24},{24,20},{28,16},{1,13},{... | collective-permute-start | bytes 786440 | tf_op jit(solution)/shard_map/ppermute | solution.py:22
  130.1 14.1 %collective-permute-start.159 = (f32[512,128]{1,0:T(8,128)}, f32[512,128]{1,0:T(8,128)S(1)}, u32[]{:S(2)}, u32[]{:S(2)}) collective-permute-start(f32[512,128]{1,0:T(8,128)} %bitcast.197), channel_id=1, source_target_pairs={{0,16},{4,20},{8,24},{12,28},{16,0},{20,4},{24,8},{28,12},{1,17},{... | collective-permute-start | bytes 786440 | tf_op jit(solution)/shard_map/ppermute | solution.py:22
  132.2 23.6 %collective-permute-start.160 = (f32[512,128]{1,0:T(8,128)}, f32[512,128]{1,0:T(8,128)S(1)}, u32[]{:S(2)}, u32[]{:S(2)}) collective-permute-start(f32[512,128]{1,0:T(8,128)} %bitcast.196), channel_id=1, source_target_pairs={{0,20},{4,16},{8,28},{12,24},{16,4},{20,0},{24,12},{28,8},{1,21},{... | collective-permute-start | bytes 786440 | tf_op jit(solution)/shard_map/ppermute | solution.py:22
  132.2 26.1 %collective-permute-start.161 = (f32[512,128]{1,0:T(8,128)}, f32[512,128]{1,0:T(8,128)S(1)}, u32[]{:S(2)}, u32[]{:S(2)}) collective-permute-start(f32[512,128]{1,0:T(8,128)} %bitcast.195), channel_id=1, source_target_pairs={{0,24},{4,28},{8,16},{12,20},{16,8},{20,12},{24,0},{28,4},{1,25},{... | collective-permute-start | bytes 786440 | tf_op jit(solution)/shard_map/ppermute | solution.py:22
  137.7 20.5 %collective-permute-start.162 = (f32[512,128]{1,0:T(8,128)}, f32[512,128]{1,0:T(8,128)S(1)}, u32[]{:S(2)}, u32[]{:S(2)}) collective-permute-start(f32[512,128]{1,0:T(8,128)} %bitcast.194), channel_id=1, source_target_pairs={{0,28},{4,24},{8,20},{12,16},{16,12},{20,8},{24,4},{28,0},{1,29},{... | collective-permute-start | bytes 786440 | tf_op jit(solution)/shard_map/ppermute | solution.py:22
  142.2 23.1 %collective-permute-start.135 = (f32[256,256]{1,0:T(8,128)}, f32[256,256]{1,0:T(8,128)S(1)}, u32[]{:S(2)}, u32[]{:S(2)}) collective-permute-start(f32[256,256]{1,0:T(8,128)} %get-tuple-element.1311), channel_id=1, source_target_pairs={{0,1},{1,0},{2,3},{3,2},{4,5},{5,4},{6,7},{7,6},{8,9},{9,8},{10,11... | collective-permute-start | bytes 786440 | tf_op jit(solution)/shard_map/ppermute | solution.py:22
  144.2 22.8 %collective-permute-start.136 = (f32[256,256]{1,0:T(8,128)}, f32[256,256]{1,0:T(8,128)S(1)}, u32[]{:S(2)}, u32[]{:S(2)}) collective-permute-start(f32[256,256]{1,0:T(8,128)} %get-tuple-element.1310), channel_id=1, source_target_pairs={{0,2},{1,3},{2,0},{3,1},{4,6},{5,7},{6,4},{7,5},{8,10},{9,11},{10,... | collective-permute-start | bytes 786440 | tf_op jit(solution)/shard_map/ppermute | solution.py:22
  155.7 12.8 %collective-permute-start.137 = (f32[256,256]{1,0:T(8,128)}, f32[256,256]{1,0:T(8,128)}, u32[]{:S(2)}, u32[]{:S(2)}) collective-permute-start(f32[256,256]{1,0:T(8,128)} %get-tuple-element.1309), channel_id=1, source_target_pairs={{0,3},{1,2},{2,1},{3,0},{4,7},{5,6},{6,5},{7,4},{8,11},{9,10},{10,... | collective-permute-start | bytes 786440 | tf_op jit(solution)/shard_map/ppermute | solution.py:22
  165.1 3.8 %collective-permute-start.163 = (f32[512,128]{1,0:T(8,128)S(1)}, f32[512,128]{1,0:T(8,128)S(1)}, u32[]{:S(2)}, u32[]{:S(2)}) collective-permute-start(f32[512,128]{1,0:T(8,128)S(1)} %get-tuple-element.821), channel_id=1, source_target_pairs={{0,4},{4,0},{8,12},{12,8},{16,20},{20,16},{24,28},{28,24},{1,5},{5... | collective-permute-start | bytes 786440 | tf_op jit(solution)/shard_map/ppermute | solution.py:22
  165.3 9.2 %collective-permute-start.164 = (f32[512,128]{1,0:T(8,128)S(1)}, f32[512,128]{1,0:T(8,128)S(1)}, u32[]{:S(2)}, u32[]{:S(2)}) collective-permute-start(f32[512,128]{1,0:T(8,128)S(1)} %get-tuple-element.822), channel_id=1, source_target_pairs={{0,8},{4,12},{8,0},{12,4},{16,24},{20,28},{24,16},{28,20},{1,9},{5... | collective-permute-start | bytes 786440 | tf_op jit(solution)/shard_map/ppermute | solution.py:22
  165.4 14.0 %collective-permute-start.165 = (f32[512,128]{1,0:T(8,128)S(1)}, f32[512,128]{1,0:T(8,128)S(1)}, u32[]{:S(2)}, u32[]{:S(2)}) collective-permute-start(f32[512,128]{1,0:T(8,128)S(1)} %get-tuple-element.823), channel_id=1, source_target_pairs={{0,12},{4,8},{8,4},{12,0},{16,28},{20,24},{24,20},{28,16},{1,13},{... | collective-permute-start | bytes 786440 | tf_op jit(solution)/shard_map/ppermute | solution.py:22
  167.0 14.4 %collective-permute-start.166 = (f32[512,128]{1,0:T(8,128)S(1)}, f32[512,128]{1,0:T(8,128)S(1)}, u32[]{:S(2)}, u32[]{:S(2)}) collective-permute-start(f32[512,128]{1,0:T(8,128)S(1)} %get-tuple-element.824), channel_id=1, source_target_pairs={{0,16},{4,20},{8,24},{12,28},{16,0},{20,4},{24,8},{28,12},{1,17},{... | collective-permute-start | bytes 786440 | tf_op jit(solution)/shard_map/ppermute | solution.py:22
  168.5 23.5 %collective-permute-start.167 = (f32[512,128]{1,0:T(8,128)S(1)}, f32[512,128]{1,0:T(8,128)S(1)}, u32[]{:S(2)}, u32[]{:S(2)}) collective-permute-start(f32[512,128]{1,0:T(8,128)S(1)} %get-tuple-element.825), channel_id=1, source_target_pairs={{0,20},{4,16},{8,28},{12,24},{16,4},{20,0},{24,12},{28,8},{1,21},{... | collective-permute-start | bytes 786440 | tf_op jit(solution)/shard_map/ppermute | solution.py:22
  168.9 24.5 %collective-permute-start.168 = (f32[512,128]{1,0:T(8,128)S(1)}, f32[512,128]{1,0:T(8,128)S(1)}, u32[]{:S(2)}, u32[]{:S(2)}) collective-permute-start(f32[512,128]{1,0:T(8,128)S(1)} %get-tuple-element.826), channel_id=1, source_target_pairs={{0,24},{4,28},{8,16},{12,20},{16,8},{20,12},{24,0},{28,4},{1,25},{... | collective-permute-start | bytes 786440 | tf_op jit(solution)/shard_map/ppermute | solution.py:22
  174.5 18.9 %collective-permute-start.169 = (f32[512,128]{1,0:T(8,128)S(1)}, f32[512,128]{1,0:T(8,128)S(1)}, u32[]{:S(2)}, u32[]{:S(2)}) collective-permute-start(f32[512,128]{1,0:T(8,128)S(1)} %get-tuple-element.827), channel_id=1, source_target_pairs={{0,28},{4,24},{8,20},{12,16},{16,12},{20,8},{24,4},{28,0},{1,29},{... | collective-permute-start | bytes 786440 | tf_op jit(solution)/shard_map/ppermute | solution.py:22
  179.3 16.0 %collective-permute-start.150 = (f32[256,256]{1,0:T(8,128)S(1)}, f32[256,256]{1,0:T(8,128)S(1)}, u32[]{:S(2)}, u32[]{:S(2)}) collective-permute-start(f32[256,256]{1,0:T(8,128)S(1)} %get-tuple-element.809), channel_id=1, source_target_pairs={{0,1},{1,0},{2,3},{3,2},{4,5},{5,4},{6,7},{7,6},{8,9},{9,8},{10,11... | collective-permute-start | bytes 786440 | tf_op jit(solution)/shard_map/ppermute | solution.py:22
  181.4 15.4 %collective-permute-start.151 = (f32[256,256]{1,0:T(8,128)S(1)}, f32[256,256]{1,0:T(8,128)S(1)}, u32[]{:S(2)}, u32[]{:S(2)}) collective-permute-start(f32[256,256]{1,0:T(8,128)S(1)} %get-tuple-element.810), channel_id=1, source_target_pairs={{0,2},{1,3},{2,0},{3,1},{4,6},{5,7},{6,4},{7,5},{8,10},{9,11},{10,... | collective-permute-start | bytes 786440 | tf_op jit(solution)/shard_map/ppermute | solution.py:22
  192.0 10.7 %collective-permute-start.152 = (f32[256,256]{1,0:T(8,128)S(1)}, f32[256,256]{1,0:T(8,128)S(1)}, u32[]{:S(2)}, u32[]{:S(2)}) collective-permute-start(f32[256,256]{1,0:T(8,128)S(1)} %get-tuple-element.811), channel_id=1, source_target_pairs={{0,3},{1,2},{2,1},{3,0},{4,7},{5,6},{6,5},{7,4},{8,11},{9,10},{10,... | collective-permute-start | bytes 786440 | tf_op jit(solution)/shard_map/ppermute | solution.py:22
  (1 other events, 5.8 us)
where the time goes:
time: 208 us; the launch traced here: 205 us
  waiting for transfers between devices  103 us (50%)
  starting transfers between devices  55.1 us (26%)
  Pallas kernels  35.7 us (17%)
  local copies, waits for them, and re-layouts  5.91 us (3%)
  between operations  2.44 us (1%)
    ppermute x44, waiting for transfers between devices, exchange(): return lax.ppermute(value, axis, [(i, i ^ bits) for i in range(size)])  103 us
    ppermute x44, starting transfers between devices, exchange(): return lax.ppermute(value, axis, [(i, i ^ bits) for i in range(size)])  55.1 us
    pallas_call x3, Pallas kernels, turn(): pl.pallas_call(functools.partial(turn_kernel, masked, n_col), in_specs=[S...  14.6 us
    pallas_call x1, Pallas kernels, reflect(): pl.pallas_call(functools.partial(reflect_kernel, [(r, k) for _, r, k in p...  7.88 us
    pallas_call x1, Pallas kernels, stand(): pl.pallas_call(functools.partial(stand_kernel, n_row, count), in_specs=[S...  6.81 us
    pallas_call x3, Pallas kernels, place(): pl.pallas_call(functools.partial(place_kernel, groups, axis, tail), in_sp...  6.44 us
  transfers between devices with their start and end apart: 44, of which 18 were waited for; matrix products, arithmetic and copies ran while one was open for 3% of the time, Pallas kernels for 11%

commit v1 on v0

--- a/solution.py
+++ b/solution.py
@@ -9,8 +9,10 @@
 
 
 LEVELS = 60
+FRONT = 3
+PARTS = 4
 TILE = 256
-VMEM_LIMIT = 48 * 1024 * 1024
+VMEM_LIMIT = 20 * 1024 * 1024
 VMEM = pl.BlockSpec(memory_space=pltpu.VMEM)
 SMEM = pl.BlockSpec(memory_space=pltpu.SMEM)
 ANY = pl.BlockSpec(memory_space=pl.ANY)
@@ -29,6 +31,11 @@
 
 def dot(a, b):
     return jnp.dot(a, b, preferred_element_type=F32)
+
+
+def below(bound, period, block, position):
+    full = lax.div(bound, jnp.int32(period))
+    return full * block + jnp.clip(bound - full * period - position * block, 0, block)
 
 
 def gather_factor(factor, n_row, n_col):
@@ -61,13 +68,14 @@
     return pieces
 
 
-def reflect_kernel(places, block_rows, scalars, *refs):
+def reflect_kernel(places, block_rows, place_ref, deflated_ref, *refs):
     count = len(places)
     sources = refs[:count]
     high_ref, low_ref = refs[count : count + 2]
     (vector_ref,) = refs[count + 2 :]
-    row_position, col_position, kept_count = scalars[0], scalars[1], scalars[2]
-    n_col, _, local_width = high_ref.shape
+    row_position, col_position = place_ref[0], place_ref[1]
+    n_col, width, local_width = high_ref.shape
+    kept_count = width - deflated_ref[0]
     groups = {}
     for source, (row_bits, col_bits) in zip(sources, places):
         groups.setdefault(row_bits, []).append((source, col_bits))
@@ -113,25 +121,27 @@
             lax.fori_loop(0, source.shape[0], write_step, 0)
 
 
-def reflect(pieces, scalars, n_row, n_col, block_rows, local_width):
+def reflect(pieces, position, deflated, n_row, n_col, block_rows, local_width):
     natural = jax.ShapeDtypeStruct((n_col, n_row * block_rows, local_width), BF16)
     return pl.pallas_call(
         functools.partial(reflect_kernel, [(r, k) for _, r, k in pieces], block_rows),
-        in_specs=[SMEM] + [VMEM] * len(pieces),
+        in_specs=[SMEM] * 2 + [VMEM] * len(pieces),
         out_specs=[VMEM] * 2,
         out_shape=[natural, natural],
         scratch_shapes=[pltpu.VMEM((n_col, 1, local_width), F32)],
         compiler_params=pltpu.CompilerParams(vmem_limit_bytes=VMEM_LIMIT),
         name="reflect",
-    )(scalars, *[a for a, _, _ in pieces])
-
-
-def turn_kernel(masked, n_col, scalars, *refs):
+    )(position, deflated, *[a for a, _, _ in pieces])
+
+
+def turn_kernel(n_col, bound, place_ref, *refs):
+    if bound is not None:
+        start_ref, *refs = refs
     sources = refs[:n_col]
     high_ref, low_ref = refs[n_col : n_col + 2]
     outs = refs[n_col + 2 : 2 * n_col + 2]
     stacked, result = refs[2 * n_col + 2 :]
-    position, threshold = scalars[0], scalars[1]
+    position = place_ref[1]
     rows, local_width = sources[0].shape
     for k in range(n_col):
         high, low = split(sources[k][...])
@@ -149,20 +159,23 @@
         return carry
 
     lax.fori_loop(0, n_col, column_step, 0)
+    if bound is not None:
+        threshold = below(start_ref[0], *bound, place_ref[0]) - position * rows
     for k in range(n_col):
         turned = result[k]
-        if masked:
+        if bound is not None:
             number = lax.broadcasted_iota(jnp.int32, (rows, local_width), 0)
             turned = jnp.where(number < threshold, turned, sources[k][...])
         outs[k][...] = turned
 
 
-def turn(sources, high, low, scalars, masked):
+def turn(sources, high, low, position, start=None, bound=None):
     n_col = len(sources)
     rows, local_width = sources[0].shape
+    small = [position] if bound is None else [position, start]
     return pl.pallas_call(
-        functools.partial(turn_kernel, masked, n_col),
-        in_specs=[SMEM] + [VMEM] * (n_col + 2),
+        functools.partial(turn_kernel, n_col, bound),
+        in_specs=[SMEM] * len(small) + [VMEM] * (n_col + 2),
         out_specs=[VMEM] * n_col,
         out_shape=[jax.ShapeDtypeStruct((rows, local_width), F32)] * n_col,
         scratch_shapes=[
@@ -171,15 +184,76 @@
         ],
         compiler_params=pltpu.CompilerParams(vmem_limit_bytes=VMEM_LIMIT),
         name="turn",
-    )(scalars, *sources, high, low)
-
-
-def stand_kernel(n_row, count, scalars, *refs):
+    )(*small, *sources, high, low)
+
+
+def lead_kernel(n_col, place_ref, *refs):
+    sources = refs[:n_col]
+    high_ref, low_ref, out, stacked = refs[n_col:]
+    position = place_ref[1]
+    rows, _ = sources[0].shape
+    for k in range(n_col):
+        high, low = split(sources[k][...])
+        stacked[position ^ k, :rows, :] = high
+        stacked[position ^ k, rows:, :] = low
+    out[...] = column_of(position ^ (n_col - 1), stacked, high_ref, low_ref)
+
+
+def column_of(column, stacked, high_ref, low_ref):
+    n_col, double, local_width = stacked.shape
+    rows = double // 2
+    total = jnp.zeros((rows, local_width), F32)
+    for k in range(n_col):
+        band = pl.ds(k * local_width, local_width)
+        both = dot(stacked[k], high_ref[column, band, :])
+        total = total + both[rows:] + dot(stacked[k, :rows, :], low_ref[column, band, :]) + both[:rows]
+    return total
+
+
+def follow_kernel(n_col, place_ref, stacked, high_ref, low_ref, *refs):
+    outs, result = refs[:-1], refs[-1]
+    position = place_ref[1]
+
+    def column_step(j, carry):
+        result[j] = column_of(position ^ j, stacked, high_ref, low_ref)
+        return carry
+
+    lax.fori_loop(0, n_col - 1, column_step, 0)
+    for k in range(n_col - 1):
+        outs[k][...] = result[k]
+
+
+def turn_in_two(sources, high, low, position):
+    n_col = len(sources)
+    rows, local_width = sources[0].shape
+    piece = jax.ShapeDtypeStruct((rows, local_width), F32)
+    params = pltpu.CompilerParams(vmem_limit_bytes=VMEM_LIMIT)
+    last, stacked = pl.pallas_call(
+        functools.partial(lead_kernel, n_col),
+        in_specs=[SMEM] + [VMEM] * (n_col + 2),
+        out_specs=[VMEM] * 2,
+        out_shape=[piece, jax.ShapeDtypeStruct((n_col, 2 * rows, local_width), BF16)],
+        compiler_params=params,
+        name="lead",
+    )(position, *sources, high, low)
+    others = pl.pallas_call(
+        functools.partial(follow_kernel, n_col),
+        in_specs=[SMEM] + [VMEM] * 3,
+        out_specs=[VMEM] * (n_col - 1),
+        out_shape=[piece] * (n_col - 1),
+        scratch_shapes=[pltpu.VMEM((n_col - 1, rows, local_width), F32)],
+        compiler_params=params,
+        name="follow",
+    )(position, stacked, high, low)
+    return list(others) + [last]
+
+
+def stand_kernel(n_row, count, bound, place_ref, start_ref, *refs):
     sources = refs[:n_row]
     high_ref, low_ref = refs[n_row : n_row + 2]
     outs = refs[n_row + 2 : 2 * n_row + 2]
     panel_high, panel_low, result = refs[2 * n_row + 2 :]
-    position, threshold = scalars[0], scalars[1]
+    position = place_ref[0]
     n_col, width, local_width = high_ref.shape
     lanes = sources[0].shape[1]
     block_rows = sources[0].shape[0] // count
@@ -202,6 +276,7 @@
 
     lax.fori_loop(0, n_col, rows_step, 0)
     lane = lax.broadcasted_iota(jnp.int32, (block_rows, lanes), 1)
+    threshold = below(start_ref[0] + width, *bound, place_ref[1]) - position * (count * lanes)
     for i in range(n_row):
         rows = pl.ds(pl.multiple_of((position ^ i) * block_rows, block_rows), block_rows)
         for t in range(count):
@@ -213,13 +288,13 @@
             )
 
 
-def stand(sources, high, low, scalars, count):
+def stand(sources, high, low, position, start, count, bound):
     n_row = len(sources)
     shape = sources[0].shape
     width = high.shape[1]
     return pl.pallas_call(
-        functools.partial(stand_kernel, n_row, count),
-        in_specs=[SMEM] + [VMEM] * (n_row + 2),
+        functools.partial(stand_kernel, n_row, count, bound),
+        in_specs=[SMEM] * 2 + [VMEM] * (n_row + 2),
         out_specs=[VMEM] * n_row,
         out_shape=[jax.ShapeDtypeStruct(shape, F32)] * n_row,
         scratch_shapes=[
@@ -229,66 +304,106 @@
         ],
         compiler_params=pltpu.CompilerParams(vmem_limit_bytes=VMEM_LIMIT),
         name="stand",
-    )(scalars, *sources, high, low)
-
-
-def place_kernel(groups, axis, tail, scalars, *refs):
-    count = sum(len(g) for g in groups)
-    pieces = refs[:count]
-    position = scalars[0]
-    if tail is None:
-        target, sems = refs[count:]
-    else:
-        source, target, sems, kept, tail_sem = refs[count:]
-        keep = pl.ds(tail, target.shape[0] - tail)
-        fetch = pltpu.make_async_copy(source.at[keep], kept, tail_sem)
-        fetch.start()
+    )(position, start, *sources, high, low)
+
+
+def place_kernel(plans, counts, place_ref, *refs):
+    targets, sems = refs[-1 - len(plans) : -1], refs[-1]
     copies = []
-    for piece, (base, bits) in zip(pieces, [p for g in groups for p in g]):
-        size = piece.shape[axis]
+    first = 0
+    for number, ((groups, axis, which), target) in enumerate(zip(plans, targets)):
+        position = place_ref[which]
+        spots = [spot for group in groups for spot in group]
+        for piece, (base, bits) in zip(refs[first : first + counts[number]], spots):
+            size = piece.shape[axis]
+            start = base + (position ^ bits) * size
+            if axis == 0 and size % 8 == 0 and base % 8 == 0:
+                start = pl.multiple_of(start, 8)
+            spot = (slice(None),) * axis + (pl.ds(start, size),)
+            copies.append(pltpu.make_async_copy(piece, target.at[spot], sems.at[len(copies)]))
+        first += counts[number]
+    for copy in copies:
+        copy.start()
+    for copy in copies:
+        copy.wait()
+
+
+def place(plans, pieces, position, shapes, begun=None):
+    operands = [piece for part in pieces for piece in part]
+    counts = [len(part) for part in pieces]
+    in_specs = [SMEM] + [VMEM] * len(operands)
+    aliases = {}
+    for number, array in (begun or {}).items():
+        aliases[1 + len(operands)] = number
+        operands.append(array)
+        in_specs.append(ANY)
+    return pl.pallas_call(
+        functools.partial(place_kernel, plans, counts),
+        in_specs=in_specs,
+        out_specs=[ANY] * len(plans),
+        out_shape=[jax.ShapeDtypeStruct(shape, F32) for shape in shapes],
+        input_output_aliases=aliases,
+        scratch_shapes=[pltpu.SemaphoreType.DMA((sum(counts),))],
+        compiler_params=pltpu.CompilerParams(vmem_limit_bytes=VMEM_LIMIT),
+        name="place",
+    )(position, *operands)
+
+
+def cut_kernel(spots, axis, which, place_ref, source, *refs):
+    outs, sems = refs[:-1], refs[-1]
+    position = place_ref[which]
+    copies = []
+    for out, (base, bits) in zip(outs, spots):
+        size = out.shape[axis]
         start = base + (position ^ bits) * size
         if axis == 0 and size % 8 == 0 and base % 8 == 0:
             start = pl.multiple_of(start, 8)
         spot = (slice(None),) * axis + (pl.ds(start, size),)
-        copies.append(pltpu.make_async_copy(piece, target.at[spot], sems.at[len(copies)]))
+        copies.append(pltpu.make_async_copy(source.at[spot], out, sems.at[len(copies)]))
     for copy in copies:
         copy.start()
-    if tail is not None:
-        fetch.wait()
-        copies.append(pltpu.make_async_copy(kept, target.at[keep], sems.at[len(copies)]))
-        copies[-1].start()
     for copy in copies:
         copy.wait()
 
 
-def place(groups, pieces, position, shape, axis=0, source=None, tail=None):
-    operands = list(pieces)
-    in_specs = [SMEM] + [VMEM] * len(pieces)
-    scratch = [pltpu.SemaphoreType.DMA((len(pieces) + 1,))]
-    if tail is not None:
-        operands.append(source)
-        in_specs.append(ANY)
-        scratch += [pltpu.VMEM((shape[0] - tail,) + shape[1:], F32), pltpu.SemaphoreType.DMA]
+def cut(source, spots, sizes, axis, which, position):
+    shapes = [source.shape[:axis] + (size,) + source.shape[axis + 1 :] for size in sizes]
     return pl.pallas_call(
-        functools.partial(place_kernel, groups, axis, tail),
-        in_specs=in_specs,
+        functools.partial(cut_kernel, spots, axis, which),
+        in_specs=[SMEM, ANY],
+        out_specs=[VMEM] * len(spots),
+        out_shape=[jax.ShapeDtypeStruct(shape, F32) for shape in shapes],
+        scratch_shapes=[pltpu.SemaphoreType.DMA((len(spots),))],
+        compiler_params=pltpu.CompilerParams(vmem_limit_bytes=VMEM_LIMIT),
+        name="cut",
+    )(position, source)
+
+
+def keep_kernel(tail, source, target, kept, sem):
+    rows = pl.ds(tail, target.shape[0] - tail)
+    for copy in (
+        pltpu.make_async_copy(source.at[rows], kept, sem),
+        pltpu.make_async_copy(kept, target.at[rows], sem),
+    ):
+        copy.start()
+        copy.wait()
+
+
+def keep(source, tail):
+    shape = source.shape
+    return pl.pallas_call(
+        functools.partial(keep_kernel, tail),
+        in_specs=[ANY],
         out_specs=ANY,
         out_shape=jax.ShapeDtypeStruct(shape, F32),
-        scratch_shapes=scratch,
+        scratch_shapes=[pltpu.VMEM((shape[0] - tail,) + shape[1:], F32), pltpu.SemaphoreType.DMA],
         compiler_params=pltpu.CompilerParams(vmem_limit_bytes=VMEM_LIMIT),
-        name="place",
-    )(position, *operands)
-
-
-def below(bound, period, block, position):
-    full = bound // period
-    return full * block + jnp.clip(bound - full * period - position * block, 0, block)
+        name="keep",
+    )(source)
 
 
 def body(n_row, n_col, vectors_window, column_strip, row_strip, factor, window_start, deflated):
-    row_position = lax.axis_index("row").astype(jnp.int32)
-    col_position = lax.axis_index("col").astype(jnp.int32)
-    start_row = window_start[0]
+    position = jnp.stack([lax.axis_index("row"), lax.axis_index("col")]).astype(jnp.int32)
     rounds, _, blocks, local_width = vectors_window.shape
     block_rows = factor.shape[0]
     width = block_rows * n_row
@@ -299,70 +414,66 @@
 
     pieces = gather_factor(factor, n_row, n_col)
 
-    def rows_in(matrix, base, size):
-        parts = [lax.dynamic_slice_in_dim(matrix, base + (col_position ^ k) * size, size) for k in range(n_col)]
-        order = range(n_col - 1, 0, -1)
-        got = {k: exchange(parts[k], "col", k, n_col) for k in order}
-        return [parts[0]] + [got[k] for k in range(1, n_col)]
-
-    def rows_out(parts):
+    def rows_in(parts):
         got = {k: exchange(parts[k], "col", k, n_col) for k in range(n_col - 1, 0, -1)}
         return [parts[0]] + [got[k] for k in range(1, n_col)]
 
-    half = height // 2
-    share = half // n_col
-    first_in = rows_in(vectors, 0, share)
-    second_in = rows_in(vectors, half, share)
+    front = height * FRONT // PARTS
+    sizes = [front // n_col] * n_col + [(height - front) // n_col] * n_col
+    spots = [(0, k) for k in range(n_col)] + [(front, k) for k in range(n_col)]
+    cuts = cut(vectors, spots, sizes, 0, 1, position)
+    first_in = rows_in(cuts[:n_col])
+    second_in = rows_in(cuts[n_col:])
     per_device = col_rounds // n_row
     piece_shape = (strip_rows, per_device, 1, col_block)
     flat_shape = (strip_rows * per_device, col_block)
-    row_parts = [
-        lax.dynamic_slice_in_dim(row_strip, (row_position ^ i) * per_device, per_device, axis=1).reshape(flat_shape)
-        for i in range(n_row)
-    ]
+    cuts = cut(row_strip, [(0, i) for i in range(n_row)], [per_device] * n_row, 1, 0, position)
+    row_parts = [part.reshape(flat_shape) for part in cuts]
     row_in = [row_parts[0]] + [exchange(row_parts[i], "row", i, n_row) for i in range(1, n_row)]
 
-    scalars = jnp.stack([row_position, col_position, width - deflated[0]])
-    high, low = reflect(pieces, scalars, n_row, n_col, block_rows, local_width)
-
-    col_scalars = jnp.stack([col_position, jnp.int32(0)])
-    first_turned = turn(first_in, high, low, col_scalars, False)
-    first_out = rows_out(first_turned)
-    second_turned = turn(second_in, high, low, col_scalars, False)
-
-    columns_kept = below(start_row + width, n_col * col_block, col_block, col_position)
-    row_scalars = jnp.stack([row_position, columns_kept - row_position * (per_device * col_block)])
-    stood = stand(row_in, high, low, row_scalars, per_device)
+    high, low = reflect(pieces, position, deflated, n_row, n_col, block_rows, local_width)
+
+    first_turned = turn_in_two(first_in, high, low, position)
+    first_out = rows_in(first_turned)
+    second_turned = turn(second_in, high, low, position)
+    bound = (n_col * col_block, col_block)
+    stood = stand(row_in, high, low, position, window_start, per_device, bound)
     row_out = [stood[0]] + [exchange(stood[i], "row", i, n_row) for i in range(1, n_row)]
 
     round_rows = n_row * blocks
     active_rounds = -(-(rounds * round_rows - width) // round_rows)
     levels = min(LEVELS // n_col, active_rounds)
-    rows_turned = below(start_row, round_rows, blocks, row_position)
     sizes = [-(-active_rounds * (level + 1) // levels) for level in range(levels)]
 
-    def branch(index, strip, high, low, rows_turned, *second):
+    def branch(index, strip, high, low, position, start, *second):
         used = sizes[index]
         size = used * blocks // n_col
-        strip_in = rows_in(strip, 0, size)
-        second_out = rows_out(list(second))
-        strip_scalars = jnp.stack([col_position, rows_turned - col_position * size])
-        turned = turn(strip_in, high, low, strip_scalars, True)
-        strip_out = rows_out(turned)
+        cuts = cut(strip, [(0, k) for k in range(n_col)], [size] * n_col, 0, 1, position)
+        strip_in = rows_in(cuts)
+        second_out = rows_in(list(second))
+        turned = turn(strip_in, high, low, position, start, (round_rows, blocks))
+        strip_out = rows_in(turned)
+        begun = None
+        if used < rounds:
+            begun = {0: keep(strip, used * blocks)}
         groups = [[(0, k) for k in range(n_col)]]
-        tail = used * blocks if used < rounds else None
-        updated = place(groups, strip_out, col_scalars, strip.shape, source=strip, tail=tail)
-        return [updated] + second_out
-
-    used_rounds = -(-start_row // round_rows)
-    level = sum((used_rounds > size).astype(jnp.int32) for size in sizes[:-1]) if levels > 1 else jnp.int32(0)
+        (strip_updated,) = place([(groups, 0, 1)], [strip_out], position, [strip.shape], begun)
+        return [strip_updated] + second_out
+
+    ends = jnp.asarray([size * round_rows for size in sizes[:-1]] or [rounds * round_rows], jnp.int32)
+    level = jnp.sum((window_start > ends).astype(jnp.int32))
+    branches = [functools.partial(branch, i) for i in range(levels)]
     strip_updated, *second_out = lax.switch(
-        level, [functools.partial(branch, i) for i in range(levels)], strip, high, low, rows_turned, *second_turned
+        level, branches, strip, high, low, position, window_start, *second_turned
     )
-    groups = [[(0, k) for k in range(n_col)], [(half, k) for k in range(n_col)]]
-    vectors_updated = place(groups, first_out + second_out, col_scalars, vectors.shape)
     row_pieces = [part.reshape(piece_shape) for part in row_out]
-    row_updated = place([[(0, i) for i in range(n_row)]], row_pieces, row_scalars, row_strip.shape, axis=1)
+    vectors_updated, row_updated, strip_updated = place(
+        [([[(base, k) for k in range(n_col)] for base in (0, front)], 0, 1), ([[(0, i) for i in range(n_row)]], 1, 0), ([], 0, 0)],
+        [first_out + second_out, row_pieces, []],
+        position,
+        [vectors.shape, row_strip.shape, strip.shape],
+        {2: strip_updated},
+    )
     return (
         vectors_updated.reshape(vectors_window.shape),
         strip_updated.reshape(column_strip.shape),

time: 208 us -> 206 us (level)
  the two profiles are of different devices: /device:TPU:0 before, /device:TPU:8 now
where the time goes in v1:
time: 206 us; the launch traced here: 205 us
  waiting for transfers between devices  116 us (56%)
  starting transfers between devices  44.3 us (22%)
  Pallas kernels  34.3 us (17%)
  local copies, waits for them, and re-layouts  5.5 us (3%)
  between operations  3.11 us (2%)
    ppermute x44, waiting for transfers between devices, exchange(): return lax.ppermute(value, axis, [(i, i ^ bits) for i in range(size)])  116 us
    ppermute x44, starting transfers between devices, exchange(): return lax.ppermute(value, axis, [(i, i ^ bits) for i in range(size)])  44.3 us
    pallas_call x1, Pallas kernels, stand(): pl.pallas_call(functools.partial(stand_kernel, n_row, count, bound), in_s...  6.98 us
    pallas_call x1, Pallas kernels, reflect(): pl.pallas_call(functools.partial(reflect_kernel, [(r, k) for _, r, k in p...  6.68 us
    pallas_call x3, Pallas kernels, cut(): pl.pallas_call(functools.partial(cut_kernel, spots, axis, which), in_spec...  5.24 us
    pallas_call x2, Pallas kernels, turn(): pl.pallas_call(functools.partial(turn_kernel, n_col, bound), in_specs=[SM...  4.97 us
    pallas_call x2, Pallas kernels, place(): pl.pallas_call(functools.partial(place_kernel, plans, counts), in_specs=i...  4.54 us
    unnamed x44, local copies, waits for them, and re-layouts  4.52 us
  transfers between devices with their start and end apart: 44, of which 23 were waited for; matrix products, arithmetic and copies ran while one was open for 1% of the time, Pallas kernels for 12%

profile of v1, /device:TPU:8, one launch (start us, length us, event | category | flops | bytes accessed | tf_op | source)
XLA Modules:
  0.0 205.4 jit_solution(345017862751234527)
XLA Ops:
  0.6 1.6 collective-permute-start.139
  2.3 2.5 %collective-permute-start.138 = (f32[128,256]{1,0:T(8,128)}, f32[128,256]{1,0:T(8,128)S(1)}, u32[]{:S(2)}, u32[]{:S(2)}) collective-permute-start(f32[128,256]{1,0:T(8,128)} %param.25), channel_id=1, source_target_pairs={{0,1},{1,0},{2,3},{3,2},{4,5},{5,4},{6,7},{7,6},{8,9},{9,8},{10,11... | collective-permute-start | bytes 393224 | tf_op jit(solution)/shard_map/ppermute | solution.py:24
  4.8 4.2 %collective-permute-done.139 = f32[128,256]{1,0:T(8,128)S(1)} collective-permute-done((f32[128,256]{1,0:T(8,128)}, f32[128,256]{1,0:T(8,128)S(1)}, u32[]{:S(2)}, u32[]{:S(2)}) %collective-permute-start.139) | collective-permute-done | bytes 131104 | tf_op jit(solution)/shard_map/ppermute | solution.py:24
  9.4 2.0 collective-permute-done.138
  11.3 2.6 %collective-permute-done.140 = f32[128,256]{1,0:T(8,128)S(1)} collective-permute-done((f32[128,256]{1,0:T(8,128)S(1)}, f32[128,256]{1,0:T(8,128)S(1)}, u32[]{:S(2)}, u32[]{:S(2)}) %collective-permute-start.140) | collective-permute-done | bytes 131104 | tf_op jit(solution)/shard_map/ppermute | solution.py:24
  14.9 1.6 collective-permute-start.141
  16.4 1.5 collective-permute-start.142
  18.0 9.1 %collective-permute-done.141.refs_1_ = f32[4,128,256]{2,1,0:T(8,128)S(1)} collective-permute-done((f32[4,128,256]{2,1,0:T(8,128)S(1)}, f32[4,128,256]{2,1,0:T(8,128)S(1)}, u32[]{:S(2)}, u32[]{:S(2)}) %collective-permute-start.141) | collective-permute-done | bytes 524320 | tf_op jit(solution)/shard_map/ppermute | solution.py:24
  27.1 1.3 collective-permute-done.142.refs_2_
  30.2 1.6 collective-permute-start.144
  31.7 6.5 %collective-permute-done.143.refs_3_ = f32[2,128,256]{2,1,0:T(8,128)} collective-permute-done((f32[2,128,256]{2,1,0:T(8,128)S(1)}, f32[2,128,256]{2,1,0:T(8,128)}, u32[]{:S(2)}, u32[]{:S(2)}) %collective-permute-start.143) | collective-permute-done | bytes 262176 | tf_op jit(solution)/shard_map/ppermute | solution.py:24
  38.9 2.8 %cut.32 = (f32[384,256]{1,0:T(8,128)S(1)}, f32[384,256]{1,0:T(8,128)S(1)}, f32[384,256]{1,0:T(8,128)S(1)}, f32[384,256]{1,0:T(8,128)S(1)}, f32[128,256]{1,0:T(8,...) custom-call(s32[2]{0:T(128)S(1)} %pad_add_fusion.place_ref, f32[2048,256]{1,0:T(8,128)S(1)} %bitcast.32), custom_call_target="tpu_custom_call" | custom-call | tf_op jit(solution)/shard_map/cut/pallas_call | solution.py:371
  45.3 2.0 collective-permute-start.155
  52.7 6.7 %reflect.1 = (bf16[4,1024,256]{2,1,0:T(8,128)(2,1)S(1)}, bf16[4,1024,256]{2,1,0:T(8,128)(2,1)S(1)}) custom-call(s32[2]{0:T(128)S(1)} %pad_add_fusion.place_ref, s32[1]{0:T(128)S(6)} %copy.105.deflated_ref, f32[4,128,256]{2,1,0:T(8,128)S(1)} %pad_maximum_fusion.refs_0_, f32[4,128,256]{2,1,0:T(8,128)S(1)} %collective-permute-done.141.refs_1_, ...), custom_call_target="tpu_custom_call" | custom-call | tf_op jit(solution)/shard_map/reflect/pallas_call | solution.py:126
  59.5 2.2 %turn.31 = (f32[128,256]{1,0:T(8,128)S(1)}, f32[128,256]{1,0:T(8,128)S(1)}, f32[128,256]{1,0:T(8,128)S(1)}, f32[128,256]{1,0:T(8,128)S(1)}) custom-call(s32[2]{0:T(128)S(1)} %pad_add_fusion.place_ref, f32[128,256]{1,0:T(8,128)S(1)} %copy-done.3, f32[128,256]{1,0:T(8,128)S(1)} %collective-permute-done.153.refs_1_, ...), custom_call_target="tpu_custom_call" | custom-call | tf_op jit(solution)/shard_map/turn/pallas_call | solution.py:176
  62.6 44.1 %conditional.1 = (f32[2048,256]{1,0:T(8,128)}, f32[128,256]{1,0:T(8,128)}, f32[128,256]{1,0:T(8,128)}, f32[128,256]{1,0:T(8,128)}) conditional(s32[]{:T(128)} %clamp.3, (s32[2]{0:T(128)S(1)}, f32[2048,256]{1,0:T(8,128)S(1)}, s32[1]{0:T(128)}, bf16[4,1024,256]{2,1,0:T(8,128)(2,1)S(1)}, ...), branch_computations={%region_1.0_spmd, %region_2.0_spmd, %region_3.0_spmd, %region_4.0_... | conditional | bytes 13369736 | solution.py:466
  62.7 1.3 cut.20
  63.9 1.3 collective-permute-start.27
  66.1 1.3 collective-permute-start.29
  67.5 2.6 %collective-permute-done.27.refs_2_ = f32[128,256]{1,0:T(8,128)S(1)} collective-permute-done((f32[128,256]{1,0:T(8,128)S(1)}, f32[128,256]{1,0:T(8,128)S(1)}, u32[]{:S(2)}, u32[]{:S(2)}) %collective-permute-start.27) | collective-permute-done | bytes 131104 | tf_op jit(solution)/shard_map/cond/branch_3_fun/ppermute | solution.py:24
  70.0 5.4 %collective-permute-done.28.refs_3_ = f32[128,256]{1,0:T(8,128)S(1)} collective-permute-done((f32[128,256]{1,0:T(8,128)S(1)}, f32[128,256]{1,0:T(8,128)S(1)}, u32[]{:S(2)}, u32[]{:S(2)}) %collective-permute-start.28) | collective-permute-done | bytes 131104 | tf_op jit(solution)/shard_map/cond/branch_3_fun/ppermute | solution.py:24
  75.5 3.0 %collective-permute-done.29.refs_4_ = f32[128,256]{1,0:T(8,128)S(1)} collective-permute-done((f32[128,256]{1,0:T(8,128)S(1)}, f32[128,256]{1,0:T(8,128)S(1)}, u32[]{:S(2)}, u32[]{:S(2)}) %collective-permute-start.29) | collective-permute-done | bytes 131104 | tf_op jit(solution)/shard_map/cond/branch_3_fun/ppermute | solution.py:24
  78.5 2.8 %turn.19 = (f32[128,256]{1,0:T(8,128)S(1)}, f32[128,256]{1,0:T(8,128)S(1)}, f32[128,256]{1,0:T(8,128)S(1)}, f32[128,256]{1,0:T(8,128)S(1)}) custom-call(s32[2]{0:T(128)S(1)} %get-tuple-element.288.place_ref, s32[1]{0:T(128)} %get-tuple-element.289.refs_0_, f32[128,256]{1,0:T(8,128)S(1)} %get-tuple-element.291.refs_1_, ...), custom_call_target="tpu_custom_call" | custom-call | tf_op jit(solution)/shard_map/cond/branch_3_fun/turn/pallas_call | solution.py:176
  81.4 2.0 collective-permute-start.33
  85.0 3.3 %collective-permute-start.34 = (f32[128,256]{1,0:T(8,128)S(1)}, f32[128,256]{1,0:T(8,128)}, u32[]{:S(2)}, u32[]{:S(2)}) collective-permute-start(f32[128,256]{1,0:T(8,128)S(1)} %get-tuple-element.302), channel_id=1, source_target_pairs={{0,2},{1,3},{2,0},{3,1},{4,6},{5,7},{6,4},{7,5},{8,10},{9,11},{10,... | collective-permute-start | bytes 393224 | tf_op jit(solution)/shard_map/cond/branch_3_fun/ppermute | solution.py:24
  90.5 8.4 %collective-permute-done.31.refs_2_ = f32[128,256]{1,0:T(8,128)S(1)} collective-permute-done((f32[128,256]{1,0:T(8,128)S(1)}, f32[128,256]{1,0:T(8,128)S(1)}, u32[]{:S(2)}, u32[]{:S(2)}) %collective-permute-start.31) | collective-permute-done | bytes 131104 | tf_op jit(solution)/shard_map/cond/branch_3_fun/ppermute | solution.py:24
  99.0 4.4 %collective-permute-done.32.refs_3_ = f32[128,256]{1,0:T(8,128)S(1)} collective-permute-done((f32[128,256]{1,0:T(8,128)S(1)}, f32[128,256]{1,0:T(8,128)S(1)}, u32[]{:S(2)}, u32[]{:S(2)}) %collective-permute-start.32) | collective-permute-done | bytes 131104 | tf_op jit(solution)/shard_map/cond/branch_3_fun/ppermute | solution.py:24
  103.4 1.4 place.19
  104.8 2.0 collective-permute-done.35
  106.8 1.5 collective-permute-start.157
  108.6 1.5 collective-permute-start.159
  110.4 5.8 %collective-permute-done.157.refs_2_ = f32[512,128]{1,0:T(8,128)S(1)} collective-permute-done((f32[512,128]{1,0:T(8,128)}, f32[512,128]{1,0:T(8,128)S(1)}, u32[]{:S(2)}, u32[]{:S(2)}) %collective-permute-start.157) | collective-permute-done | bytes 262176 | tf_op jit(solution)/shard_map/ppermute | solution.py:24
  116.2 2.5 %collective-permute-start.161 = (f32[512,128]{1,0:T(8,128)}, f32[512,128]{1,0:T(8,128)S(1)}, u32[]{:S(2)}, u32[]{:S(2)}) collective-permute-start(f32[512,128]{1,0:T(8,128)} %bitcast.43), channel_id=1, source_target_pairs={{0,24},{4,28},{8,16},{12,20},{16,8},{20,12},{24,0},{28,4},{1,25},{... | collective-permute-start | bytes 786440 | tf_op jit(solution)/shard_map/ppermute | solution.py:24
  118.6 2.3 %collective-permute-done.158.refs_3_ = f32[512,128]{1,0:T(8,128)S(1)} collective-permute-done((f32[512,128]{1,0:T(8,128)}, f32[512,128]{1,0:T(8,128)S(1)}, u32[]{:S(2)}, u32[]{:S(2)}) %collective-permute-start.158) | collective-permute-done | bytes 262176 | tf_op jit(solution)/shard_map/ppermute | solution.py:24
  120.9 3.0 %collective-permute-start.162 = (f32[512,128]{1,0:T(8,128)}, f32[512,128]{1,0:T(8,128)S(1)}, u32[]{:S(2)}, u32[]{:S(2)}) collective-permute-start(f32[512,128]{1,0:T(8,128)} %bitcast.42), channel_id=1, source_target_pairs={{0,28},{4,24},{8,20},{12,16},{16,12},{20,8},{24,4},{28,0},{1,29},{... | collective-permute-start | bytes 786440 | tf_op jit(solution)/shard_map/ppermute | solution.py:24
  124.6 8.7 %collective-permute-done.160.refs_5_ = f32[512,128]{1,0:T(8,128)S(1)} collective-permute-done((f32[512,128]{1,0:T(8,128)}, f32[512,128]{1,0:T(8,128)S(1)}, u32[]{:S(2)}, u32[]{:S(2)}) %collective-permute-start.160) | collective-permute-done | bytes 262176 | tf_op jit(solution)/shard_map/ppermute | solution.py:24
  134.4 7.0 %stand.1 = (f32[512,128]{1,0:T(8,128)S(1)}, f32[512,128]{1,0:T(8,128)S(1)}, f32[512,128]{1,0:T(8,128)S(1)}, f32[512,128]{1,0:T(8,128)S(1)}, f32[512,128]{1,0:T(8...) custom-call(s32[2]{0:T(128)S(1)} %pad_add_fusion.place_ref, s32[1]{0:T(128)} %copy.104.start_ref, ...), custom_call_target="tpu_custom_call" | custom-call | tf_op jit(solution)/shard_map/stand/pallas_call | solution.py:295
  142.1 1.6 collective-permute-start.164
  143.7 7.2 %collective-permute-done.136.refs_2_ = f32[384,256]{1,0:T(8,128)S(1)} collective-permute-done((f32[384,256]{1,0:T(8,128)S(1)}, f32[384,256]{1,0:T(8,128)S(1)}, u32[]{:S(2)}, u32[]{:S(2)}) %collective-permute-start.136) | collective-permute-done | bytes 393248 | tf_op jit(solution)/shard_map/ppermute | solution.py:24
  151.4 7.7 %collective-permute-done.137.refs_3_ = f32[384,256]{1,0:T(8,128)S(1)} collective-permute-done((f32[384,256]{1,0:T(8,128)S(1)}, f32[384,256]{1,0:T(8,128)S(1)}, u32[]{:S(2)}, u32[]{:S(2)}) %collective-permute-start.137) | collective-permute-done | bytes 393248 | tf_op jit(solution)/shard_map/ppermute | solution.py:24
  159.2 1.7 lead.1
  160.9 3.0 %follow.1 = (f32[384,256]{1,0:T(8,128)S(1)}, f32[384,256]{1,0:T(8,128)S(1)}, f32[384,256]{1,0:T(8,128)S(1)}) custom-call(s32[2]{0:T(128)S(1)} %pad_add_fusion.place_ref, bf16[4,768,256]{2,1,0:T(8,128)(2,1)S(1)} %get-tuple-element.531.stacked, bf16[4,1024,256]{2,1,0:T(8,128)(2,1)S(1)} %copy-done.18, bf16[4,1024,256]{2,1,0:T(8,128)(2,1)S(1)} %copy-done.20), custom_call_target="tpu_custom_call" | custom-call | tf_op jit(solution)/shard_map/follow/pallas_call | solution.py:239
  163.9 2.5 %collective-permute-start.151 = (f32[384,256]{1,0:T(8,128)S(1)}, f32[384,256]{1,0:T(8,128)S(1)}, u32[]{:S(2)}, u32[]{:S(2)}) collective-permute-start(f32[384,256]{1,0:T(8,128)S(1)} %get-tuple-element.534), channel_id=1, source_target_pairs={{0,2},{1,3},{2,0},{3,1},{4,6},{5,7},{6,4},{7,5},{8,10},{9,11},{10,... | collective-permute-start | bytes 1179656 | tf_op jit(solution)/shard_map/ppermute | solution.py:24
  169.4 8.0 %collective-permute-done.168 = f32[512,128]{1,0:T(8,128)S(1)} collective-permute-done((f32[512,128]{1,0:T(8,128)S(1)}, f32[512,128]{1,0:T(8,128)S(1)}, u32[]{:S(2)}, u32[]{:S(2)}) %collective-permute-start.168) | collective-permute-done | bytes 262176 | tf_op jit(solution)/shard_map/ppermute | solution.py:24
  177.5 3.2 %collective-permute-done.169 = f32[512,128]{1,0:T(8,128)S(1)} collective-permute-done((f32[512,128]{1,0:T(8,128)S(1)}, f32[512,128]{1,0:T(8,128)S(1)}, u32[]{:S(2)}, u32[]{:S(2)}) %collective-permute-start.169) | collective-permute-done | bytes 262176 | tf_op jit(solution)/shard_map/ppermute | solution.py:24
  181.2 11.7 %collective-permute-done.151.refs_2_ = f32[384,256]{1,0:T(8,128)S(1)} collective-permute-done((f32[384,256]{1,0:T(8,128)S(1)}, f32[384,256]{1,0:T(8,128)S(1)}, u32[]{:S(2)}, u32[]{:S(2)}) %collective-permute-start.151) | collective-permute-done | bytes 393248 | tf_op jit(solution)/shard_map/ppermute | solution.py:24
  192.9 9.2 %collective-permute-done.152.refs_3_ = f32[384,256]{1,0:T(8,128)S(1)} collective-permute-done((f32[384,256]{1,0:T(8,128)S(1)}, f32[384,256]{1,0:T(8,128)S(1)}, u32[]{:S(2)}, u32[]{:S(2)}) %collective-permute-start.152) | collective-permute-done | bytes 393248 | tf_op jit(solution)/shard_map/ppermute | solution.py:24
  202.1 3.2 %place.31 = (f32[2048,256]{1,0:T(8,128)}, f32[128,32,1,128]{3,2,1,0:T(1,128)}, f32[2048,256]{1,0:T(8,128)}) custom-call(s32[2]{0:T(128)S(1)} %pad_add_fusion.place_ref, f32[384,256]{1,0:T(8,128)S(1)} %get-tuple-element.532.refs_0_, f32[384,256]{1,0:T(8,128)S(1)} %collective-permute-done.150.refs_1_, ...), custom_call_target="tpu_custom_call", output_to_operand_aliasing={{2}: (17, {})} | custom-call | tf_op jit(solution)/shard_map/place/pallas_call | solution.py:340
  (102 shorter events, 23.5 us)
Async XLA Ops:
  0.6 38.2 %copy-start = (f32[32,1,64,256]{3,2,1,0:T(8,128)S(1)}, f32[32,1,64,256]{3,2,1,0:T(8,128)}, u32[]{:S(2)}) copy-start(f32[32,1,64,256]{3,2,1,0:T(8,128)} %param.22) | copy-start | bytes 6291460
  0.6 8.3 %collective-permute-start.139 = (f32[128,256]{1,0:T(8,128)}, f32[128,256]{1,0:T(8,128)S(1)}, u32[]{:S(2)}, u32[]{:S(2)}) collective-permute-start(f32[128,256]{1,0:T(8,128)} %param.25), channel_id=1, source_target_pairs={{0,3},{1,2},{2,1},{3,0},{4,7},{5,6},{6,5},{7,4},{8,11},{9,10},{10,... | collective-permute-start | bytes 393224 | tf_op jit(solution)/shard_map/ppermute | solution.py:24
  2.3 9.1 %collective-permute-start.138 = (f32[128,256]{1,0:T(8,128)}, f32[128,256]{1,0:T(8,128)S(1)}, u32[]{:S(2)}, u32[]{:S(2)}) collective-permute-start(f32[128,256]{1,0:T(8,128)} %param.25), channel_id=1, source_target_pairs={{0,1},{1,0},{2,3},{3,2},{4,5},{5,4},{6,7},{7,6},{8,9},{9,8},{10,11... | collective-permute-start | bytes 393224 | tf_op jit(solution)/shard_map/ppermute | solution.py:24
  9.0 5.0 %collective-permute-start.140 = (f32[128,256]{1,0:T(8,128)S(1)}, f32[128,256]{1,0:T(8,128)S(1)}, u32[]{:S(2)}, u32[]{:S(2)}) collective-permute-start(f32[128,256]{1,0:T(8,128)S(1)} %collective-permute-done.139), channel_id=1, source_target_pairs={{0,1},{1,0},{2,3},{3,2},{4,5},{5,4},{6,7},{7,6},{8,9},{9,8},{10,11... | collective-permute-start | bytes 393224 | tf_op jit(solution)/shard_map/ppermute | solution.py:24
  14.9 12.2 %collective-permute-start.141 = (f32[4,128,256]{2,1,0:T(8,128)S(1)}, f32[4,128,256]{2,1,0:T(8,128)S(1)}, u32[]{:S(2)}, u32[]{:S(2)}) collective-permute-start(f32[4,128,256]{2,1,0:T(8,128)S(1)} %pad_maximum_fusion.refs_0_), channel_id=1, source_target_pairs={{0,8},{4,12},{8,0},{12,4},{16,24},{20,28},{24,16},{28,20},{1,9},{5... | collective-permute-start | bytes 1572872 | tf_op jit(solution)/shard_map/ppermute | solution.py:24
  16.4 12.0 %collective-permute-start.142 = (f32[4,128,256]{2,1,0:T(8,128)S(1)}, f32[4,128,256]{2,1,0:T(8,128)}, u32[]{:S(2)}, u32[]{:S(2)}) collective-permute-start(f32[4,128,256]{2,1,0:T(8,128)S(1)} %pad_maximum_fusion.refs_0_), channel_id=1, source_target_pairs={{0,16},{4,20},{8,24},{12,28},{16,0},{20,4},{24,8},{28,12},{1,17},{... | collective-permute-start | bytes 1572872 | tf_op jit(solution)/shard_map/ppermute | solution.py:24
  17.9 25.9 %collective-permute-start.145 = (f32[4,128,256]{2,1,0:T(8,128)S(1)}, f32[4,128,256]{2,1,0:T(8,128)}, u32[]{:S(2)}, u32[]{:S(2)}) collective-permute-start(f32[4,128,256]{2,1,0:T(8,128)S(1)} %pad_maximum_fusion.refs_0_), channel_id=1, source_target_pairs={{0,4},{4,0},{8,12},{12,8},{16,20},{20,16},{24,28},{28,24},{1,5},{5... | collective-permute-start | bytes 1572872 | tf_op jit(solution)/shard_map/ppermute | solution.py:24
  27.1 17.1 %collective-permute-start.146 = (f32[4,128,256]{2,1,0:T(8,128)S(1)}, f32[4,128,256]{2,1,0:T(8,128)}, u32[]{:S(2)}, u32[]{:S(2)}) collective-permute-start(f32[4,128,256]{2,1,0:T(8,128)S(1)} %collective-permute-done.141.refs_1_), channel_id=1, source_target_pairs={{0,4},{4,0},{8,12},{12,8},{16,20},{20,16},{24,28},{28,24},{1,5},{5... | collective-permute-start | bytes 1572872 | tf_op jit(solution)/shard_map/ppermute | solution.py:24
  28.4 16.9 %collective-permute-start.147 = (f32[4,128,256]{2,1,0:T(8,128)}, f32[4,128,256]{2,1,0:T(8,128)}, u32[]{:S(2)}, u32[]{:S(2)}) collective-permute-start(f32[4,128,256]{2,1,0:T(8,128)} %collective-permute-done.142.refs_2_), channel_id=1, source_target_pairs={{0,4},{4,0},{8,12},{12,8},{16,20},{20,16},{24,28},{28,24},{1,5},{5... | collective-permute-start | bytes 1572872 | tf_op jit(solution)/shard_map/ppermute | solution.py:24
  29.4 8.9 %collective-permute-start.143 = (f32[2,128,256]{2,1,0:T(8,128)S(1)}, f32[2,128,256]{2,1,0:T(8,128)}, u32[]{:S(2)}, u32[]{:S(2)}) collective-permute-start(f32[2,128,256]{2,1,0:T(8,128)S(1)} %slice.8), channel_id=1, source_target_pairs={{0,8},{4,12},{8,0},{12,4},{16,24},{20,28},{24,16},{28,20},{1,9},{5... | collective-permute-start | bytes 786440 | tf_op jit(solution)/shard_map/ppermute | solution.py:24
  30.2 8.5 %collective-permute-start.144 = (f32[2,128,256]{2,1,0:T(8,128)S(1)}, f32[2,128,256]{2,1,0:T(8,128)}, u32[]{:S(2)}, u32[]{:S(2)}) collective-permute-start(f32[2,128,256]{2,1,0:T(8,128)S(1)} %slice.9), channel_id=1, source_target_pairs={{0,16},{4,20},{8,24},{12,28},{16,0},{20,4},{24,8},{28,12},{1,17},{... | collective-permute-start | bytes 786440 | tf_op jit(solution)/shard_map/ppermute | solution.py:24
  38.3 14.4 %collective-permute-start.148 = (f32[2,128,256]{2,1,0:T(8,128)}, f32[2,128,256]{2,1,0:T(8,128)}, u32[]{:S(2)}, u32[]{:S(2)}) collective-permute-start(f32[2,128,256]{2,1,0:T(8,128)} %collective-permute-done.143.refs_3_), channel_id=1, source_target_pairs={{0,4},{4,0},{8,12},{12,8},{16,20},{20,16},{24,28},{28,24},{1,5},{5... | collective-permute-start | bytes 786440 | tf_op jit(solution)/shard_map/ppermute | solution.py:24
  38.6 14.1 %collective-permute-start.149 = (f32[2,128,256]{2,1,0:T(8,128)}, f32[2,128,256]{2,1,0:T(8,128)}, u32[]{:S(2)}, u32[]{:S(2)}) collective-permute-start(f32[2,128,256]{2,1,0:T(8,128)} %collective-permute-done.144.refs_4_), channel_id=1, source_target_pairs={{0,4},{4,0},{8,12},{12,8},{16,20},{20,16},{24,28},{28,24},{1,5},{5... | collective-permute-start | bytes 786440 | tf_op jit(solution)/shard_map/ppermute | solution.py:24
  43.9 15.6 %collective-permute-start.153 = (f32[128,256]{1,0:T(8,128)}, f32[128,256]{1,0:T(8,128)S(1)}, u32[]{:S(2)}, u32[]{:S(2)}) collective-permute-start(f32[128,256]{1,0:T(8,128)} %get-tuple-element.537), channel_id=1, source_target_pairs={{0,1},{1,0},{2,3},{3,2},{4,5},{5,4},{6,7},{7,6},{8,9},{9,8},{10,11... | collective-permute-start | bytes 393224 | tf_op jit(solution)/shard_map/ppermute | solution.py:24
  44.2 15.3 %collective-permute-start.154 = (f32[128,256]{1,0:T(8,128)}, f32[128,256]{1,0:T(8,128)S(1)}, u32[]{:S(2)}, u32[]{:S(2)}) collective-permute-start(f32[128,256]{1,0:T(8,128)} %get-tuple-element.538), channel_id=1, source_target_pairs={{0,2},{1,3},{2,0},{3,1},{4,6},{5,7},{6,4},{7,5},{8,10},{9,11},{10,... | collective-permute-start | bytes 393224 | tf_op jit(solution)/shard_map/ppermute | solution.py:24
  45.3 14.2 %collective-permute-start.155 = (f32[128,256]{1,0:T(8,128)}, f32[128,256]{1,0:T(8,128)S(1)}, u32[]{:S(2)}, u32[]{:S(2)}) collective-permute-start(f32[128,256]{1,0:T(8,128)} %get-tuple-element.539), channel_id=1, source_target_pairs={{0,3},{1,2},{2,1},{3,0},{4,7},{5,6},{6,5},{7,4},{8,11},{9,10},{10,... | collective-permute-start | bytes 393224 | tf_op jit(solution)/shard_map/ppermute | solution.py:24
  62.6 61.4 %copy-start.7 = (f32[384,256]{1,0:T(8,128)S(1)}, f32[384,256]{1,0:T(8,128)}, u32[]{:S(2)}) copy-start(f32[384,256]{1,0:T(8,128)} %copy-done.6) | copy-start | bytes 1179652
  62.6 70.7 %copy-start.5 = (f32[384,256]{1,0:T(8,128)S(1)}, f32[384,256]{1,0:T(8,128)}, u32[]{:S(2)}) copy-start(f32[384,256]{1,0:T(8,128)} %copy-done.4) | copy-start | bytes 1179652
  63.9 6.1 %collective-permute-start.27 = (f32[128,256]{1,0:T(8,128)S(1)}, f32[128,256]{1,0:T(8,128)S(1)}, u32[]{:S(2)}, u32[]{:S(2)}) collective-permute-start(f32[128,256]{1,0:T(8,128)S(1)} %get-tuple-element.292), channel_id=1, source_target_pairs={{0,1},{1,0},{2,3},{3,2},{4,5},{5,4},{6,7},{7,6},{8,9},{9,8},{10,11... | collective-permute-start | bytes 393224 | tf_op jit(solution)/shard_map/cond/branch_3_fun/ppermute | solution.py:24
  65.2 10.2 %collective-permute-start.28 = (f32[128,256]{1,0:T(8,128)S(1)}, f32[128,256]{1,0:T(8,128)S(1)}, u32[]{:S(2)}, u32[]{:S(2)}) collective-permute-start(f32[128,256]{1,0:T(8,128)S(1)} %get-tuple-element.293), channel_id=1, source_target_pairs={{0,2},{1,3},{2,0},{3,1},{4,6},{5,7},{6,4},{7,5},{8,10},{9,11},{10,... | collective-permute-start | bytes 393224 | tf_op jit(solution)/shard_map/cond/branch_3_fun/ppermute | solution.py:24
  66.1 12.4 %collective-permute-start.29 = (f32[128,256]{1,0:T(8,128)S(1)}, f32[128,256]{1,0:T(8,128)S(1)}, u32[]{:S(2)}, u32[]{:S(2)}) collective-permute-start(f32[128,256]{1,0:T(8,128)S(1)} %get-tuple-element.294), channel_id=1, source_target_pairs={{0,3},{1,2},{2,1},{3,0},{4,7},{5,6},{6,5},{7,4},{8,11},{9,10},{10,... | collective-permute-start | bytes 393224 | tf_op jit(solution)/shard_map/cond/branch_3_fun/ppermute | solution.py:24
  81.3 6.9 %collective-permute-start.30 = (f32[128,256]{1,0:T(8,128)S(1)}, f32[128,256]{1,0:T(8,128)S(1)}, u32[]{:S(2)}, u32[]{:S(2)}) collective-permute-start(f32[128,256]{1,0:T(8,128)S(1)} %get-tuple-element.298), channel_id=1, source_target_pairs={{0,1},{1,0},{2,3},{3,2},{4,5},{5,4},{6,7},{7,6},{8,9},{9,8},{10,11... | collective-permute-start | bytes 393224 | tf_op jit(solution)/shard_map/cond/branch_3_fun/ppermute | solution.py:24
  81.4 23.4 %collective-permute-start.33 = (f32[128,256]{1,0:T(8,128)S(1)}, f32[128,256]{1,0:T(8,128)}, u32[]{:S(2)}, u32[]{:S(2)}) collective-permute-start(f32[128,256]{1,0:T(8,128)S(1)} %get-tuple-element.301), channel_id=1, source_target_pairs={{0,1},{1,0},{2,3},{3,2},{4,5},{5,4},{6,7},{7,6},{8,9},{9,8},{10,11... | collective-permute-start | bytes 393224 | tf_op jit(solution)/shard_map/cond/branch_3_fun/ppermute | solution.py:24
  83.4 15.6 %collective-permute-start.31 = (f32[128,256]{1,0:T(8,128)S(1)}, f32[128,256]{1,0:T(8,128)S(1)}, u32[]{:S(2)}, u32[]{:S(2)}) collective-permute-start(f32[128,256]{1,0:T(8,128)S(1)} %get-tuple-element.299), channel_id=1, source_target_pairs={{0,2},{1,3},{2,0},{3,1},{4,6},{5,7},{6,4},{7,5},{8,10},{9,11},{10,... | collective-permute-start | bytes 393224 | tf_op jit(solution)/shard_map/cond/branch_3_fun/ppermute | solution.py:24
  83.9 19.4 %collective-permute-start.32 = (f32[128,256]{1,0:T(8,128)S(1)}, f32[128,256]{1,0:T(8,128)S(1)}, u32[]{:S(2)}, u32[]{:S(2)}) collective-permute-start(f32[128,256]{1,0:T(8,128)S(1)} %get-tuple-element.300), channel_id=1, source_target_pairs={{0,3},{1,2},{2,1},{3,0},{4,7},{5,6},{6,5},{7,4},{8,11},{9,10},{10,... | collective-permute-start | bytes 393224 | tf_op jit(solution)/shard_map/cond/branch_3_fun/ppermute | solution.py:24
  85.0 19.8 %collective-permute-start.34 = (f32[128,256]{1,0:T(8,128)S(1)}, f32[128,256]{1,0:T(8,128)}, u32[]{:S(2)}, u32[]{:S(2)}) collective-permute-start(f32[128,256]{1,0:T(8,128)S(1)} %get-tuple-element.302), channel_id=1, source_target_pairs={{0,2},{1,3},{2,0},{3,1},{4,6},{5,7},{6,4},{7,5},{8,10},{9,11},{10,... | collective-permute-start | bytes 393224 | tf_op jit(solution)/shard_map/cond/branch_3_fun/ppermute | solution.py:24
  88.3 18.5 %collective-permute-start.35 = (f32[128,256]{1,0:T(8,128)S(1)}, f32[128,256]{1,0:T(8,128)}, u32[]{:S(2)}, u32[]{:S(2)}) collective-permute-start(f32[128,256]{1,0:T(8,128)S(1)} %get-tuple-element.303), channel_id=1, source_target_pairs={{0,3},{1,2},{2,1},{3,0},{4,7},{5,6},{6,5},{7,4},{8,11},{9,10},{10,... | collective-permute-start | bytes 393224 | tf_op jit(solution)/shard_map/cond/branch_3_fun/ppermute | solution.py:24
  106.8 3.5 %collective-permute-start.156 = (f32[512,128]{1,0:T(8,128)}, f32[512,128]{1,0:T(8,128)S(1)}, u32[]{:S(2)}, u32[]{:S(2)}) collective-permute-start(f32[512,128]{1,0:T(8,128)} %bitcast.48), channel_id=1, source_target_pairs={{0,4},{4,0},{8,12},{12,8},{16,20},{20,16},{24,28},{28,24},{1,5},{5... | collective-permute-start | bytes 786440 | tf_op jit(solution)/shard_map/ppermute | solution.py:24
  106.8 9.4 %collective-permute-start.157 = (f32[512,128]{1,0:T(8,128)}, f32[512,128]{1,0:T(8,128)S(1)}, u32[]{:S(2)}, u32[]{:S(2)}) collective-permute-start(f32[512,128]{1,0:T(8,128)} %bitcast.47), channel_id=1, source_target_pairs={{0,8},{4,12},{8,0},{12,4},{16,24},{20,28},{24,16},{28,20},{1,9},{5... | collective-permute-start | bytes 786440 | tf_op jit(solution)/shard_map/ppermute | solution.py:24
  108.3 12.6 %collective-permute-start.158 = (f32[512,128]{1,0:T(8,128)}, f32[512,128]{1,0:T(8,128)S(1)}, u32[]{:S(2)}, u32[]{:S(2)}) collective-permute-start(f32[512,128]{1,0:T(8,128)} %bitcast.46), channel_id=1, source_target_pairs={{0,12},{4,8},{8,4},{12,0},{16,28},{20,24},{24,20},{28,16},{1,13},{... | collective-permute-start | bytes 786440 | tf_op jit(solution)/shard_map/ppermute | solution.py:24
  108.6 15.3 %collective-permute-start.159 = (f32[512,128]{1,0:T(8,128)}, f32[512,128]{1,0:T(8,128)S(1)}, u32[]{:S(2)}, u32[]{:S(2)}) collective-permute-start(f32[512,128]{1,0:T(8,128)} %bitcast.45), channel_id=1, source_target_pairs={{0,16},{4,20},{8,24},{12,28},{16,0},{20,4},{24,8},{28,12},{1,17},{... | collective-permute-start | bytes 786440 | tf_op jit(solution)/shard_map/ppermute | solution.py:24
  110.1 23.2 %collective-permute-start.160 = (f32[512,128]{1,0:T(8,128)}, f32[512,128]{1,0:T(8,128)S(1)}, u32[]{:S(2)}, u32[]{:S(2)}) collective-permute-start(f32[512,128]{1,0:T(8,128)} %bitcast.44), channel_id=1, source_target_pairs={{0,20},{4,16},{8,28},{12,24},{16,4},{20,0},{24,12},{28,8},{1,21},{... | collective-permute-start | bytes 786440 | tf_op jit(solution)/shard_map/ppermute | solution.py:24
  110.3 33.4 %collective-permute-start.135 = (f32[384,256]{1,0:T(8,128)}, f32[384,256]{1,0:T(8,128)S(1)}, u32[]{:S(2)}, u32[]{:S(2)}) collective-permute-start(f32[384,256]{1,0:T(8,128)} %copy-done.8), channel_id=1, source_target_pairs={{0,1},{1,0},{2,3},{3,2},{4,5},{5,4},{6,7},{7,6},{8,9},{9,8},{10,11... | collective-permute-start | bytes 1179656 | tf_op jit(solution)/shard_map/ppermute | solution.py:24
  116.2 18.2 %collective-permute-start.161 = (f32[512,128]{1,0:T(8,128)}, f32[512,128]{1,0:T(8,128)S(1)}, u32[]{:S(2)}, u32[]{:S(2)}) collective-permute-start(f32[512,128]{1,0:T(8,128)} %bitcast.43), channel_id=1, source_target_pairs={{0,24},{4,28},{8,16},{12,20},{16,8},{20,12},{24,0},{28,4},{1,25},{... | collective-permute-start | bytes 786440 | tf_op jit(solution)/shard_map/ppermute | solution.py:24
  120.9 13.5 %collective-permute-start.162 = (f32[512,128]{1,0:T(8,128)}, f32[512,128]{1,0:T(8,128)S(1)}, u32[]{:S(2)}, u32[]{:S(2)}) collective-permute-start(f32[512,128]{1,0:T(8,128)} %bitcast.42), channel_id=1, source_target_pairs={{0,28},{4,24},{8,20},{12,16},{16,12},{20,8},{24,4},{28,0},{1,29},{... | collective-permute-start | bytes 786440 | tf_op jit(solution)/shard_map/ppermute | solution.py:24
  124.0 27.0 %collective-permute-start.136 = (f32[384,256]{1,0:T(8,128)S(1)}, f32[384,256]{1,0:T(8,128)S(1)}, u32[]{:S(2)}, u32[]{:S(2)}) collective-permute-start(f32[384,256]{1,0:T(8,128)S(1)} %copy-done.7), channel_id=1, source_target_pairs={{0,2},{1,3},{2,0},{3,1},{4,6},{5,7},{6,4},{7,5},{8,10},{9,11},{10,... | collective-permute-start | bytes 1179656 | tf_op jit(solution)/shard_map/ppermute | solution.py:24
  133.3 25.8 %collective-permute-start.137 = (f32[384,256]{1,0:T(8,128)S(1)}, f32[384,256]{1,0:T(8,128)S(1)}, u32[]{:S(2)}, u32[]{:S(2)}) collective-permute-start(f32[384,256]{1,0:T(8,128)S(1)} %copy-done.5), channel_id=1, source_target_pairs={{0,3},{1,2},{2,1},{3,0},{4,7},{5,6},{6,5},{7,4},{8,11},{9,10},{10,... | collective-permute-start | bytes 1179656 | tf_op jit(solution)/shard_map/ppermute | solution.py:24
  134.4 24.8 %copy-start.18 = (bf16[4,1024,256]{2,1,0:T(8,128)(2,1)S(1)}, bf16[4,1024,256]{2,1,0:T(8,128)(2,1)}, u32[]{:S(2)}) copy-start(bf16[4,1024,256]{2,1,0:T(8,128)(2,1)} %copy-done.17) | copy-start | bytes 6291460
  141.4 22.5 %collective-permute-start.163 = (f32[512,128]{1,0:T(8,128)S(1)}, f32[512,128]{1,0:T(8,128)S(1)}, u32[]{:S(2)}, u32[]{:S(2)}) collective-permute-start(f32[512,128]{1,0:T(8,128)S(1)} %get-tuple-element.556), channel_id=1, source_target_pairs={{0,4},{4,0},{8,12},{12,8},{16,20},{20,16},{24,28},{28,24},{1,5},{5... | collective-permute-start | bytes 786440 | tf_op jit(solution)/shard_map/ppermute | solution.py:24
  142.1 21.8 %collective-permute-start.164 = (f32[512,128]{1,0:T(8,128)S(1)}, f32[512,128]{1,0:T(8,128)S(1)}, u32[]{:S(2)}, u32[]{:S(2)}) collective-permute-start(f32[512,128]{1,0:T(8,128)S(1)} %get-tuple-element.557), channel_id=1, source_target_pairs={{0,8},{4,12},{8,0},{12,4},{16,24},{20,28},{24,16},{28,20},{1,9},{5... | collective-permute-start | bytes 786440 | tf_op jit(solution)/shard_map/ppermute | solution.py:24
  143.7 22.8 %collective-permute-start.165 = (f32[512,128]{1,0:T(8,128)S(1)}, f32[512,128]{1,0:T(8,128)S(1)}, u32[]{:S(2)}, u32[]{:S(2)}) collective-permute-start(f32[512,128]{1,0:T(8,128)S(1)} %get-tuple-element.558), channel_id=1, source_target_pairs={{0,12},{4,8},{8,4},{12,0},{16,28},{20,24},{24,20},{28,16},{1,13},{... | collective-permute-start | bytes 786440 | tf_op jit(solution)/shard_map/ppermute | solution.py:24
  150.9 16.5 %collective-permute-start.166 = (f32[512,128]{1,0:T(8,128)S(1)}, f32[512,128]{1,0:T(8,128)S(1)}, u32[]{:S(2)}, u32[]{:S(2)}) collective-permute-start(f32[512,128]{1,0:T(8,128)S(1)} %get-tuple-element.559), channel_id=1, source_target_pairs={{0,16},{4,20},{8,24},{12,28},{16,0},{20,4},{24,8},{28,12},{1,17},{... | collective-permute-start | bytes 786440 | tf_op jit(solution)/shard_map/ppermute | solution.py:24
  159.2 9.4 %collective-permute-start.167 = (f32[512,128]{1,0:T(8,128)S(1)}, f32[512,128]{1,0:T(8,128)S(1)}, u32[]{:S(2)}, u32[]{:S(2)}) collective-permute-start(f32[512,128]{1,0:T(8,128)S(1)} %get-tuple-element.560), channel_id=1, source_target_pairs={{0,20},{4,16},{8,28},{12,24},{16,4},{20,0},{24,12},{28,8},{1,21},{... | collective-permute-start | bytes 786440 | tf_op jit(solution)/shard_map/ppermute | solution.py:24
  163.8 17.3 %collective-permute-start.150 = (f32[384,256]{1,0:T(8,128)S(1)}, f32[384,256]{1,0:T(8,128)S(1)}, u32[]{:S(2)}, u32[]{:S(2)}) collective-permute-start(f32[384,256]{1,0:T(8,128)S(1)} %get-tuple-element.533), channel_id=1, source_target_pairs={{0,1},{1,0},{2,3},{3,2},{4,5},{5,4},{6,7},{7,6},{8,9},{9,8},{10,11... | collective-permute-start | bytes 1179656 | tf_op jit(solution)/shard_map/ppermute | solution.py:24
  163.9 28.9 %collective-permute-start.151 = (f32[384,256]{1,0:T(8,128)S(1)}, f32[384,256]{1,0:T(8,128)S(1)}, u32[]{:S(2)}, u32[]{:S(2)}) collective-permute-start(f32[384,256]{1,0:T(8,128)S(1)} %get-tuple-element.534), channel_id=1, source_target_pairs={{0,2},{1,3},{2,0},{3,1},{4,6},{5,7},{6,4},{7,5},{8,10},{9,11},{10,... | collective-permute-start | bytes 1179656 | tf_op jit(solution)/shard_map/ppermute | solution.py:24
  166.5 35.6 %collective-permute-start.152 = (f32[384,256]{1,0:T(8,128)S(1)}, f32[384,256]{1,0:T(8,128)S(1)}, u32[]{:S(2)}, u32[]{:S(2)}) collective-permute-start(f32[384,256]{1,0:T(8,128)S(1)} %get-tuple-element.535), channel_id=1, source_target_pairs={{0,3},{1,2},{2,1},{3,0},{4,7},{5,6},{6,5},{7,4},{8,11},{9,10},{10,... | collective-permute-start | bytes 1179656 | tf_op jit(solution)/shard_map/ppermute | solution.py:24
  167.4 10.1 %collective-permute-start.168 = (f32[512,128]{1,0:T(8,128)S(1)}, f32[512,128]{1,0:T(8,128)S(1)}, u32[]{:S(2)}, u32[]{:S(2)}) collective-permute-start(f32[512,128]{1,0:T(8,128)S(1)} %get-tuple-element.561), channel_id=1, source_target_pairs={{0,24},{4,28},{8,16},{12,20},{16,8},{20,12},{24,0},{28,4},{1,25},{... | collective-permute-start | bytes 786440 | tf_op jit(solution)/shard_map/ppermute | solution.py:24
  168.5 12.2 %collective-permute-start.169 = (f32[512,128]{1,0:T(8,128)S(1)}, f32[512,128]{1,0:T(8,128)S(1)}, u32[]{:S(2)}, u32[]{:S(2)}) collective-permute-start(f32[512,128]{1,0:T(8,128)S(1)} %get-tuple-element.562), channel_id=1, source_target_pairs={{0,28},{4,24},{8,20},{12,16},{16,12},{20,8},{24,4},{28,0},{1,29},{... | collective-permute-start | bytes 786440 | tf_op jit(solution)/shard_map/ppermute | solution.py:24
  (18 other events, 118.1 us)
